TPU v7x, 32 devices: a whole 2x2x4 slice. The times are simulated.
32 devices in a mesh: dp: 4 (over z), row: 4 (over x, core), col: 2 (over y).
Axes of the slice: x: 2, y: 2, z: 4, core: 2. Of those that a mesh axis runs over, the one named last changes fastest.
Arguments:
- tokens: float32 [768, 8192], P('row', ('dp', 'col')), may hold values from -6 to 6
- cotangent: float32 [768, 8192], P('row', ('dp', 'col')), may hold values from -6 to 6
- offsets: int32 [8, 2], P(('dp', 'col')), may hold values from 0 to 10
- ln1_gain: float32 [768], replicated, may hold values from 0.5 to 1.5
- ln1_bias: float32 [768], replicated, may hold values from -4 to 4
- q_weight: float32 [768, 768], P('row', 'col'), may hold values from -0.21875 to 0.21875
- k_weight: float32 [768, 768], P('row', 'col'), may hold values from -0.21875 to 0.21875
- v_weight: float32 [768, 768], P('row', 'col'), may hold values from -0.21875 to 0.21875
- q_bias: float32 [768], replicated, may hold values from -4 to 4
- v_bias: float32 [768], replicated, may hold values from -4 to 4
- rel_pos_h: float32 [27, 64], replicated, may hold values from -1.5 to 1.5
- rel_pos_w: float32 [27, 64], replicated, may hold values from -1.5 to 1.5
- out_weight: float32 [768, 768], P('row', 'col'), may hold values from -1.5 to 1.5
- out_bias: float32 [768], replicated, may hold values from -4 to 4
- ln2_gain: float32 [768], replicated, may hold values from 0.5 to 1.5
- ln2_bias: float32 [768], replicated, may hold values from -4 to 4
- up_weight: float32 [768, 3072], P('row', 'col'), may hold values from -0.21875 to 0.21875
- up_bias: float32 [3072], replicated, may hold values from -6 to 6
- down_weight: float32 [3072, 768], P('row', 'col'), may hold values from -0.109375 to 0.109375
- down_bias: float32 [768], replicated, may hold values from -4 to 4
Outputs:
- output: float32 [768, 8192], P('row', ('dp', 'col'))
- input_grad: float32 [768, 8192], P('row', ('dp', 'col'))
- ln1_gain_grad: float32 [768], replicated
- ln1_bias_grad: float32 [768], replicated
- q_weight_grad: float32 [768, 768], P('row', 'col')
- k_weight_grad: float32 [768, 768], P('row', 'col')
- v_weight_grad: float32 [768, 768], P('row', 'col')
- q_bias_grad: float32 [768], replicated
- v_bias_grad: float32 [768], replicated
- rel_pos_h_grad: float32 [27, 64], replicated
- rel_pos_w_grad: float32 [27, 64], replicated
- out_weight_grad: float32 [768, 768], P('row', 'col')
- out_bias_grad: float32 [768], replicated
- ln2_gain_grad: float32 [768], replicated
- ln2_bias_grad: float32 [768], replicated
- up_weight_grad: float32 [768, 3072], P('row', 'col')
- up_bias_grad: float32 [3072], replicated
- down_weight_grad: float32 [3072, 768], P('row', 'col')
- down_bias_grad: float32 [768], replicated
Inputs may be any that keep to these rules, and one draw needn't show every extreme that they name: `offsets`: row and column of each image's first token inside its padded grid of 42 x 42 cells.
All inputs are finite; a program needn't handle non-finite values.
Results may differ from a plain program's by a relative error of at most 0.012.
The roundings to bfloat16 on the way count: a program that leaves them out, or rounds other values in their place, can miss the bound.
Values may be sent and summed in bfloat16 or wider, within the bound.
A program may use at most 128 MiB of HBM per device.

v0:
```python
from functools import partial

import jax
import jax.numpy as jnp
from jax import lax
from jax.sharding import PartitionSpec as P

D = 768
HEAD_DIM = 64
MLP = 3072
WIN = 14
SIDE = 32
PSIDE = 42


epsilon = 1e-06
MASKED = -1e30
HIGHEST = lax.Precision.HIGHEST


def product(first_op, second_op):
    return jnp.dot(first_op, second_op, preferred_element_type=jnp.float32)


def contract_rows(first_op, second_op):
    return lax.dot_general(
        first_op, second_op, (((0,), (0,)), ((), ())), preferred_element_type=jnp.float32
    )


def contract_cols(first_op, second_op):
    return lax.dot_general(
        first_op, second_op, (((1,), (1,)), ((), ())), preferred_element_type=jnp.float32
    )


def own_block(vector, length, position):
    return lax.dynamic_slice_in_dim(vector, position * length, length, 0)


def spread_out(portion, whole_size, position):
    empty_vector = jnp.zeros((whole_size,), jnp.float32)
    return lax.dynamic_update_slice_in_dim(empty_vector, portion, position * portion.shape[0], 0)


def to_windows(source, offset):
    channels = source.shape[-1]
    blocks_side = PSIDE // WIN
    image_grid = source.reshape(SIDE, SIDE, channels)
    padded = jnp.zeros((PSIDE, PSIDE, channels), source.dtype)
    padded = lax.dynamic_update_slice(padded, image_grid, (offset[0], offset[1], jnp.int32(0)))
    blocks = padded.reshape(blocks_side, WIN, blocks_side, WIN, channels).transpose(0, 2, 1, 3, 4)
    return blocks.reshape(blocks_side * blocks_side, WIN * WIN, channels)


def from_windows(blocks, offset):
    channels = blocks.shape[-1]
    blocks_side = PSIDE // WIN
    padded = blocks.reshape(blocks_side, blocks_side, WIN, WIN, channels).transpose(0, 2, 1, 3, 4)
    padded = padded.reshape(PSIDE, PSIDE, channels)
    image_grid = lax.dynamic_slice(
        padded, (offset[0], offset[1], jnp.int32(0)), (SIDE, SIDE, channels)
    )
    return image_grid.reshape(SIDE * SIDE, channels)


def key_valid(offset):
    blocks_side = PSIDE // WIN
    coords = jnp.arange(PSIDE, dtype=jnp.int32)
    in_rows = (coords >= offset[0]) & (coords < offset[0] + SIDE)
    in_cols = (coords >= offset[1]) & (coords < offset[1] + SIDE)
    usable = (in_rows[:, None] & in_cols[None, :]).astype(jnp.int32)
    usable = usable.reshape(blocks_side, WIN, blocks_side, WIN).transpose(0, 2, 1, 3)
    return usable.reshape(blocks_side * blocks_side, WIN * WIN)


def one_hot_table():
    coords = jnp.arange(WIN, dtype=jnp.int32)
    rel_index = coords[:, None] - coords[None, :] + WIN - 1
    return (
        rel_index[:, :, None] == jnp.arange(2 * WIN - 1, dtype=jnp.int32)[None, None, :]
    ).astype(jnp.float32)


def key_maps():
    cells = jnp.arange(WIN * WIN, dtype=jnp.int32)
    coords = jnp.arange(WIN, dtype=jnp.int32)
    rows_map = (cells[None, :] // WIN == coords[:, None]).astype(jnp.float32)
    cols_map = (cells[None, :] % WIN == coords[:, None]).astype(jnp.float32)
    return (rows_map, cols_map)


def rel_table(rel_pos):
    return jnp.einsum(
        "ijr,rc->ijc", one_hot_table(), rel_pos.astype(jnp.float32), precision=HIGHEST
    )


def rel_untable(table_grad):
    return jnp.einsum("ijr,ijc->rc", one_hot_table(), table_grad, precision=HIGHEST)


def windowed(source, offset):
    head_count = source.shape[1] // HEAD_DIM
    blocks = to_windows(source, offset)
    return blocks.reshape(blocks.shape[0], WIN * WIN, head_count, HEAD_DIM)


def window_scores(query_win, key_win, table_rows, table_cols, usable):
    window_count = query_win.shape[0]
    head_count = query_win.shape[2]
    rows_map, cols_map = key_maps()
    direct = jnp.einsum(
        "nqhc,nkhc->nhqk", query_win, key_win, preferred_element_type=jnp.float32
    ) * HEAD_DIM ** (-0.5)
    query_grid = query_win.reshape(window_count, WIN, WIN, head_count, HEAD_DIM)
    along_rows = jnp.einsum(
        "nyxhc,ykc->nhyxk", query_grid, table_rows, preferred_element_type=jnp.float32
    )
    along_cols = jnp.einsum(
        "nyxhc,xkc->nhyxk", query_grid, table_cols, preferred_element_type=jnp.float32
    )
    along_rows = along_rows.reshape(window_count, head_count, WIN * WIN, WIN)
    along_cols = along_cols.reshape(window_count, head_count, WIN * WIN, WIN)
    scores = direct + jnp.einsum("nhqu,uk->nhqk", along_rows, rows_map, precision=HIGHEST)
    scores = scores + jnp.einsum("nhqw,wk->nhqk", along_cols, cols_map, precision=HIGHEST)
    return jnp.where(usable[:, None, None, :] > 0, scores, MASKED)


def attend(query_img, key_img, value_img, offset, table_rows, table_cols):
    query_win = windowed(query_img, offset)
    key_win = windowed(key_img, offset)
    value_win = windowed(value_img, offset)
    scores = window_scores(query_win, key_win, table_rows, table_cols, key_valid(offset))
    largest = jnp.max(scores, axis=-1, keepdims=True)
    log_total = largest + jnp.log(jnp.sum(jnp.exp(scores - largest), axis=-1, keepdims=True))
    weights = jnp.exp(scores - log_total).astype(jnp.bfloat16)
    mixed = jnp.einsum("nhqk,nkhc->nqhc", weights, value_win, preferred_element_type=jnp.float32)
    mixed = mixed.reshape(mixed.shape[0], WIN * WIN, query_img.shape[1])
    return (from_windows(mixed, offset).astype(jnp.bfloat16), log_total)


def attend_back(query_img, key_img, value_img, grad_img, log_total, offset, table_rows, table_cols):
    query_win = windowed(query_img, offset)
    key_win = windowed(key_img, offset)
    value_win = windowed(value_img, offset)
    grad_win = windowed(grad_img, offset)
    window_count = query_win.shape[0]
    head_count = query_win.shape[2]
    scale = HEAD_DIM ** (-0.5)
    rows_map, cols_map = key_maps()
    scores = window_scores(query_win, key_win, table_rows, table_cols, key_valid(offset))
    weights = jnp.exp(scores - log_total)
    weights_low = weights.astype(jnp.bfloat16)
    value_grad = jnp.einsum(
        "nhqk,nqhc->nkhc", weights_low, grad_win, preferred_element_type=jnp.float32
    )
    weight_grad = jnp.einsum(
        "nqhc,nkhc->nhqk", grad_win, value_win, preferred_element_type=jnp.float32
    )
    centre = jnp.sum(weights * weight_grad, axis=-1, keepdims=True)
    score_grad = (weights * (weight_grad - centre)).astype(jnp.bfloat16)
    query_grad = (
        jnp.einsum("nhqk,nkhc->nqhc", score_grad, key_win, preferred_element_type=jnp.float32)
        * scale
    )
    key_grad = (
        jnp.einsum("nhqk,nqhc->nkhc", score_grad, query_win, preferred_element_type=jnp.float32)
        * scale
    )
    along_rows = jnp.einsum(
        "nhqk,uk->nhqu",
        score_grad,
        rows_map.astype(jnp.bfloat16),
        preferred_element_type=jnp.float32,
    )
    along_cols = jnp.einsum(
        "nhqk,wk->nhqw",
        score_grad,
        cols_map.astype(jnp.bfloat16),
        preferred_element_type=jnp.float32,
    )
    along_rows = along_rows.reshape(window_count, head_count, WIN, WIN, WIN)
    along_cols = along_cols.reshape(window_count, head_count, WIN, WIN, WIN)
    rel_query = jnp.einsum(
        "nhyxk,ykc->nyxhc", along_rows, table_rows.astype(jnp.float32), precision=HIGHEST
    )
    rel_query = rel_query + jnp.einsum(
        "nhyxk,xkc->nyxhc", along_cols, table_cols.astype(jnp.float32), precision=HIGHEST
    )
    query_grad = query_grad + rel_query.reshape(window_count, WIN * WIN, head_count, HEAD_DIM)
    query_grid = query_win.reshape(window_count, WIN, WIN, head_count, HEAD_DIM).astype(jnp.float32)
    table_rows_grad = jnp.einsum("nhyxk,nyxhc->ykc", along_rows, query_grid, precision=HIGHEST)
    table_cols_grad = jnp.einsum("nhyxk,nyxhc->xkc", along_cols, query_grid, precision=HIGHEST)

    def unwindow(window_grad):
        return from_windows(
            window_grad.reshape(window_count, WIN * WIN, head_count * HEAD_DIM), offset
        )

    return (
        unwindow(query_grad),
        unwindow(key_grad),
        unwindow(value_grad),
        table_rows_grad,
        table_cols_grad,
    )


def moments(source):
    totals = lax.psum((jnp.sum(source, axis=1), jnp.sum(source * source, axis=1)), "row")
    average = totals[0][:, None] / D
    spread = totals[1][:, None] / D - average * average
    return (average, lax.rsqrt(spread + epsilon))


def norm_back(upstream, normed, inverse, gain):
    scaled = upstream * gain
    totals = lax.psum((jnp.sum(scaled, axis=1), jnp.sum(scaled * normed, axis=1)), "row")
    return inverse * (scaled - totals[0][:, None] / D - normed * totals[1][:, None] / D)


def sum_rows(stacked):
    return lax.psum_scatter(stacked, "row", scatter_dimension=2, tiled=True)


def gather_grads(stacked):
    return lax.all_gather(stacked, "row", axis=2, tiled=True)


def local(
    tokens,
    cotangent,
    offsets,
    ln1_gain,
    ln1_bias,
    q_weight,
    k_weight,
    v_weight,
    q_bias,
    v_bias,
    rel_pos_h,
    rel_pos_w,
    out_weight,
    out_bias,
    ln2_gain,
    ln2_bias,
    up_weight,
    up_bias,
    down_weight,
    down_bias,
):
    token_rows = tokens.T
    upstream_rows = cotangent.T
    row_count = lax.axis_size("row")
    row_place = lax.axis_index("row")
    col_count = lax.axis_size("col")
    col_place = lax.axis_index("col")
    own_width = token_rows.shape[1]
    hidden_width = MLP // row_count
    images = offsets.shape[0]
    local_tokens = token_rows.shape[0]
    shape_img = (images, SIDE * SIDE, own_width)
    w_query, w_key, w_value, w_out, w_up, w_down = (
        lax.all_gather(q_weight.astype(jnp.bfloat16), "col", axis=1, tiled=True),
        lax.all_gather(k_weight.astype(jnp.bfloat16), "col", axis=1, tiled=True),
        lax.all_gather(v_weight.astype(jnp.bfloat16), "col", axis=1, tiled=True),
        lax.all_gather(out_weight.astype(jnp.bfloat16), "col", axis=1, tiled=True),
        lax.all_gather(up_weight.astype(jnp.bfloat16), "col", axis=1, tiled=True),
        lax.all_gather(down_weight.astype(jnp.bfloat16), "col", axis=1, tiled=True),
    )
    first_gain = own_block(ln1_gain, own_width, row_place)
    first_shift = own_block(ln1_bias, own_width, row_place)
    second_gain = own_block(ln2_gain, own_width, row_place)
    second_shift = own_block(ln2_bias, own_width, row_place)
    b_query = own_block(q_bias, own_width, row_place)
    b_value = own_block(v_bias, own_width, row_place)
    b_out = own_block(out_bias, own_width, row_place)
    b_down = own_block(down_bias, own_width, row_place)
    b_up = own_block(up_bias, hidden_width, row_place)
    table_rows = rel_table(rel_pos_h.astype(jnp.bfloat16)).astype(jnp.bfloat16)
    table_cols = rel_table(rel_pos_w.astype(jnp.bfloat16)).astype(jnp.bfloat16)
    first_mean, first_inverse = moments(token_rows)
    first_norm = (token_rows - first_mean) * first_inverse
    first_in = (first_norm * first_gain + first_shift).astype(jnp.bfloat16)
    projected = sum_rows(
        jnp.stack(
            [product(first_in, w_query), product(first_in, w_key), product(first_in, w_value)]
        )
    )
    query_rows = (projected[0] + b_query).astype(jnp.bfloat16)
    key_rows = projected[1].astype(jnp.bfloat16)
    value_rows = (projected[2] + b_value).astype(jnp.bfloat16)

    def forward_image(pieces):
        return attend(pieces[0], pieces[1], pieces[2], pieces[3], table_rows, table_cols)

    query_img = query_rows.reshape(shape_img)
    key_img = key_rows.reshape(shape_img)
    value_img = value_rows.reshape(shape_img)
    attended_img, log_total = lax.map(forward_image, (query_img, key_img, value_img, offsets))
    attended = attended_img.reshape(local_tokens, own_width)
    branch_one = sum_rows(product(attended, w_out)[None])[0] + b_out
    middle = token_rows + branch_one
    second_mean, second_inverse = moments(middle)
    second_norm = (middle - second_mean) * second_inverse
    second_in = (second_norm * second_gain + second_shift).astype(jnp.bfloat16)
    hidden_pre = (
        lax.psum_scatter(product(second_in, w_up), "row", scatter_dimension=1, tiled=True) + b_up
    )
    gelu_exact = partial(jax.nn.gelu, approximate=False)
    hidden_act, gelu_pull = jax.vjp(gelu_exact, hidden_pre)
    hidden_low = hidden_act.astype(jnp.bfloat16)
    branch_two = sum_rows(product(hidden_low, w_down)[None])[0] + b_down
    output = middle + branch_two
    upstream_low = upstream_rows.astype(jnp.bfloat16)
    upstream_full = gather_grads(upstream_low[None])[0]
    grad_down = contract_rows(hidden_low, upstream_full)
    grad_down_bias = jnp.sum(upstream_low, axis=0, dtype=jnp.float32)
    grad_hidden = contract_cols(upstream_full, w_down)
    grad_pre = gelu_pull(grad_hidden)[0].astype(jnp.bfloat16)
    grad_up_bias = jnp.sum(grad_pre, axis=0, dtype=jnp.float32)
    grad_pre_full = lax.all_gather(grad_pre, "row", axis=1, tiled=True)
    grad_up = contract_rows(second_in, grad_pre_full)
    grad_second = contract_cols(grad_pre_full, w_up)
    second_gain_grad = jnp.sum(grad_second * second_norm, axis=0)
    second_shift_grad = jnp.sum(grad_second, axis=0)
    grad_middle = upstream_rows + norm_back(grad_second, second_norm, second_inverse, second_gain)
    grad_branch = grad_middle.astype(jnp.bfloat16)
    grad_out_bias = jnp.sum(grad_branch, axis=0, dtype=jnp.float32)
    grad_branch_full = gather_grads(grad_branch[None])[0]
    grad_out = contract_rows(attended, grad_branch_full)
    grad_attended = contract_cols(grad_branch_full, w_out).astype(jnp.bfloat16)

    def backward_image(pieces):
        return attend_back(
            pieces[0], pieces[1], pieces[2], pieces[3], pieces[4], pieces[5], table_rows, table_cols
        )

    query_grads, key_grads, value_grads, rows_grads, cols_grads = lax.map(
        backward_image,
        (query_img, key_img, value_img, grad_attended.reshape(shape_img), log_total, offsets),
    )
    query_low = query_grads.reshape(local_tokens, own_width).astype(jnp.bfloat16)
    key_low = key_grads.reshape(local_tokens, own_width).astype(jnp.bfloat16)
    value_low = value_grads.reshape(local_tokens, own_width).astype(jnp.bfloat16)
    grad_query_bias = jnp.sum(query_low, axis=0, dtype=jnp.float32)
    grad_value_bias = jnp.sum(value_low, axis=0, dtype=jnp.float32)
    projected_grads = gather_grads(jnp.stack([query_low, key_low, value_low]))
    grad_query = contract_rows(first_in, projected_grads[0])
    grad_key = contract_rows(first_in, projected_grads[1])
    grad_value = contract_rows(first_in, projected_grads[2])
    grad_first = contract_cols(projected_grads[0], w_query) + contract_cols(
        projected_grads[1], w_key
    )
    grad_first = grad_first + contract_cols(projected_grads[2], w_value)
    first_gain_grad = jnp.sum(grad_first * first_norm, axis=0)
    first_shift_grad = jnp.sum(grad_first, axis=0)
    input_grad = grad_middle + norm_back(grad_first, first_norm, first_inverse, first_gain)
    summed = lax.psum(
        (grad_query, grad_key, grad_value, grad_out, grad_up, grad_down), ("dp", "col")
    )
    own_grads = [
        lax.dynamic_slice_in_dim(
            matrix, col_place * (matrix.shape[1] // col_count), matrix.shape[1] // col_count, 1
        )
        for matrix in summed
    ]
    minor_grads = lax.psum(
        (
            spread_out(first_gain_grad, D, row_place),
            spread_out(first_shift_grad, D, row_place),
            spread_out(grad_query_bias, D, row_place),
            spread_out(grad_value_bias, D, row_place),
            rel_untable(jnp.sum(rows_grads, axis=0)),
            rel_untable(jnp.sum(cols_grads, axis=0)),
            spread_out(grad_out_bias, D, row_place),
            spread_out(second_gain_grad, D, row_place),
            spread_out(second_shift_grad, D, row_place),
            spread_out(grad_up_bias, MLP, row_place),
            spread_out(grad_down_bias, D, row_place),
        ),
        ("dp", "row", "col"),
    )
    return (
        output.T,
        input_grad.T,
        minor_grads[0],
        minor_grads[1],
        own_grads[0],
        own_grads[1],
        own_grads[2],
        minor_grads[2],
        minor_grads[3],
        minor_grads[4],
        minor_grads[5],
        own_grads[3],
        minor_grads[6],
        minor_grads[7],
        minor_grads[8],
        own_grads[4],
        minor_grads[9],
        own_grads[5],
        minor_grads[10],
    )


def solution(mesh):
    placed = (
        P("row", ("dp", "col")),
        P("row", ("dp", "col")),
        P(("dp", "col"), None),
        P(),
        P(),
        P("row", "col"),
        P("row", "col"),
        P("row", "col"),
        P(),
        P(),
        P(),
        P(),
        P("row", "col"),
        P(),
        P(),
        P(),
        P("row", "col"),
        P(),
        P("row", "col"),
        P(),
    )
    return jax.shard_map(
        local,
        mesh=mesh,
        in_specs=placed,
        out_specs=(
            P("row", ("dp", "col")),
            P("row", ("dp", "col")),
            P(),
            P(),
            P("row", "col"),
            P("row", "col"),
            P("row", "col"),
            P(),
            P(),
            P(),
            P(),
            P("row", "col"),
            P(),
            P(),
            P(),
            P("row", "col"),
            P(),
            P("row", "col"),
            P(),
        ),
        check_vma=False,
    )
```

profile of v0, /device:TPU:0, one launch (start us, length us, event | category | flops | bytes accessed | tf_op | source)
XLA Modules:
  0.0 1063.6 jit_solution(14196740586454919692)
XLA Ops:
  13.1 7.5 all_gather.30
  21.7 5.8 all_gather.31
  27.5 5.8 all_gather.32
  33.4 5.7 all-reduce.7
  41.3 4.2 pad_maximum_fusion
  45.5 14.4 %copy.166 = f32[3,1024,768]{1,0,2:T(4,128)} copy(f32[3,1024,768]{2,1,0:T(8,128)} %pad_maximum_fusion) | data formatting | bytes 18874368
  59.9 17.5 %copy.173 = f32[96,8,3,1024]{3,1,2,0:T(8,128)} copy(f32[96,8,3,1024]{3,2,1,0:T(4,128)} %bitcast.212) | data formatting | bytes 18874368
  86.9 6.4 all_gather.33
  94.5 62.7 %reduce-scatter.7.cloned.1.call-done = f32[192,3072]{1,0:T(8,128)} async-done(((f32[768,3072]{1,0:T(8,128)}), f32[192,3072]{1,0:T(8,128)}) %reduce-scatter.7.cloned.1.call-update) | async-done | bytes 2359312
  157.2 5.0 reshape.431
  165.7 5.3 fusion.80
  183.0 4.9 reshape.394
  191.8 5.8 dynamic_update_slice.69
  202.2 4.6 reshape.396
  214.6 5.5 dynamic_update_slice.67
  224.8 4.6 reshape.392
  232.0 3.8 copy.109
  235.8 6.1 convolution_bitcast_fusion.5
  241.9 5.7 copy.115
  284.7 8.5 copy.120
  302.8 60.8 %all-reduce.12.cloned.1.call-done = f32[1,1024,768]{1,0,2:T(1,128)} async-done(((f32[1,1024,768]{1,0,2:T(1,128)}), f32[1,1024,768]{1,0,2:T(1,128)}) %all-reduce.12.cloned.1.call-update) | async-done | bytes 3145744
  365.5 12.7 %all-reduce.6 = (f32[1024]{0:T(1024)S(1)}, f32[1024]{0:T(1024)S(1)}) all-reduce(f32[1024]{0:T(1024)S(1)} %get-tuple-element.135, f32[1024]{0:T(1024)S(1)} %get-tuple-element.134), channel_id=1, replica_groups=mesh['dp'=4,'row'=4,'col'=2] {'row'}, use_global_device_ids=true, to_apply=%region_11.12 | all-reduce | flops 2048 | bytes 16384 | tf_op jit(solution)/shard_map/psum | solution.py:211
  378.3 7.7 fusion.76
  386.9 96.4 %reduce-scatter.5.cloned.1.call-done = f32[1024,768]{1,0:T(8,128)} async-done(((f32[1024,3072]{1,0:T(8,128)}), f32[1024,768]{1,0:T(8,128)}) %reduce-scatter.5.cloned.1.call-update) | async-done | bytes 3145744 | tf_op jit(solution)/shard_map/reduce_scatter | solution.py:309
  483.3 12.4 %convert_reduce_fusion = (f32[768]{0:T(1024)}, bf16[1024,768]{1,0:T(8,128)(2,1)}, f32[1024,768]{1,0:T(8,128)S(1)}) fusion(f32[1024,768]{1,0:T(8,128)} %reduce-scatter.5.cloned.1.call-done, f32[768]{0:T(1024)S(1)} %dynamic_slice.92, bf16[1024,768]{0,1:T(8,128)(2,1)} %all-gather.17.cloned.1.call-done, bf16[768,768]{1,0:T(8,128)(2,1)} %all-gather.11.cloned.1.call-done), kind=kOutput, calls=%fused_computation.9 | convolution fusion | flops 1266941184 | bytes 10622976 | tf_op jit(solution)/shard_map/dot_general | solution.py:32
  500.4 8.5 copy.121
  510.9 66.6 %all-reduce.14.cloned.1.call-done = f32[1,1024,768]{1,0,2:T(1,128)} async-done(((f32[1,1024,768]{1,0,2:T(1,128)}), f32[1,1024,768]{1,0,2:T(1,128)}) %all-reduce.14.cloned.1.call-update) | async-done | bytes 3145744
  579.2 46.2 %all-gather.13.cloned.1.call-done = bf16[1024,3072]{1,0:T(8,128)(2,1)} async-done(((bf16[1024,768]{1,0:T(8,128)(2,1)}), bf16[1024,3072]{1,0:T(8,128)(2,1)}) %all-gather.13.cloned.1.call-update) | async-done | bytes 6291472 | tf_op jit(solution)/shard_map/all_gather | solution.py:323
  625.5 6.6 multiply_reduce_fusion.1
  632.1 6.1 all-reduce.5
  641.8 20.6 %all-gather.19.cloned.1.call-done = bf16[1024,768]{0,1:T(8,128)(2,1)} async-done(((bf16[1024,192]{0,1:T(8,128)(2,1)}), bf16[1024,768]{0,1:T(8,128)(2,1)}) %all-gather.19.cloned.1.call-update) | async-done | bytes 1572880 | tf_op jit(solution)/shard_map/all_gather | solution.py:228
  672.9 4.7 convolution_bitcast_fusion.7
  677.6 4.2 multiply_reduce_fusion
  691.6 4.7 reshape.412
  709.3 4.7 reshape.410
  730.0 6.1 copy.131
  736.0 3.7 fusion.83
  739.8 4.0 bitcast_add_fusion
  745.9 4.1 reshape.407
  767.0 4.3 fusion.85
  771.3 6.3 fusion.75
  779.1 25.4 %all-gather.15.cloned.1.call-done = bf16[3,1024,768]{1,2,0:T(8,128)(2,1)} async-done(((bf16[3,1024,192]{1,2,0:T(8,128)(2,1)}), bf16[3,1024,768]{1,2,0:T(8,128)(2,1)}) %all-gather.15.cloned.1.call-update) | async-done | bytes 4718608 | tf_op jit(solution)/shard_map/all_gather | solution.py:228
  815.3 6.1 copy.150
  821.9 5.1 fusion.29
  827.4 5.1 fusion.26
  839.6 45.1 %all-reduce.2 = (f32[768]{0:T(1024)}, f32[768]{0:T(1024)}, f32[768]{0:T(1024)}, f32[768]{0:T(1024)}, f32[27,64]{1,0:T(8,128)}, /*index=5*/f32[27,64]{1,0:T(8,128...) all-reduce(f32[768]{0:T(1024)S(1)} %dynamic_update_slice.71, ...), channel_id=1, replica_groups=mesh['dp'=4,'row'=4,'col'=2] {'dp','row','col'}, use_global_device_ids=true, to_apply=%region_24.25 | all-reduce | flops 12672 | bytes 101376 | tf_op jit(solution)/shard_map/psum | solution.py:369
  884.7 7.1 all-reduce.4
  892.9 153.0 %all-reduce.16.cloned.1.call-done = (f32[192,768]{1,0:T(8,128)}, f32[192,768]{1,0:T(8,128)}, f32[192,768]{1,0:T(8,128)}, f32[192,768]{1,0:T(8,128)}, f32[192,3072]{1,0:T(8,128)}, /*index=5*/f32[768,768]{1,0:T(8,128)}) async-done(((f32[192,768]{1,0:T(8,128)}, f32[192,768]{1,0:T(8,128)}, f32[192,768]{1,0:T(8,128)}, f32[192,768]{1,0:T(8,128)}, f32[192,3072]{1,0:T(8,128)}, /*index=5*/f32[768,768]{1,0:T(8,128)}), ...) | async-done | bytes 7077904 | tf_op jit(solution)/shard_map/psum | solution.py:360
  (314 shorter events, 213.0 us)
Async XLA Ops:
  8.0 31.1 %copy-start.5 = (f32[192,1024]{1,0:T(8,128)S(1)}, f32[192,1024]{1,0:T(8,128)}, u32[]{:S(2)}) copy-start(f32[192,1024]{1,0:T(8,128)} %param.20) | copy-start | bytes 2359300
  8.0 19.5 %copy-start.40 = (f32[192,384]{1,0:T(8,128)S(1)}, f32[192,384]{1,0:T(8,128)}, u32[]{:S(2)}) copy-start(f32[192,384]{1,0:T(8,128)} %param.27) | copy-start | bytes 884740
  8.0 149.1 %reduce-scatter.7.cloned.1.call-start = ((), (), s32[]{:S(2)}) async-start(), calls=%async_computation.9 | async-start | bytes 11796480
  9.0 31.1 %copy-start.52 = (f32[192]{0:T(256)}, f32[192]{0:T(256)S(1)}, u32[]{:S(2)}) copy-start(f32[192]{0:T(256)S(1)} %dynamic_slice.84) | copy-start | bytes 2308
  20.6 20.0 %copy-start.22 = (bf16[192,768]{1,0:T(8,128)(2,1)}, bf16[192,768]{1,0:T(8,128)(2,1)S(1)}, u32[]{:S(2)}) copy-start(bf16[192,768]{1,0:T(8,128)(2,1)S(1)} %all_gather.30) | copy-start | bytes 884740
  27.5 13.1 %copy-start.24 = (bf16[192,768]{1,0:T(8,128)(2,1)}, bf16[192,768]{1,0:T(8,128)(2,1)S(1)}, u32[]{:S(2)}) copy-start(bf16[192,768]{1,0:T(8,128)(2,1)S(1)} %all_gather.31) | copy-start | bytes 884740
  33.4 7.3 copy-start.30
  77.4 8.2 copy-start.41
  77.4 16.0 %copy-start.67 = (f32[27,64]{1,0:T(8,128)S(1)}, f32[27,64]{1,0:T(8,128)}, u32[]{:S(2)}) copy-start(f32[27,64]{1,0:T(8,128)} %param.31) | copy-start | bytes 20740
  77.4 16.9 %copy-start.68 = (f32[27,64]{1,0:T(8,128)S(1)}, f32[27,64]{1,0:T(8,128)}, u32[]{:S(2)}) copy-start(f32[27,64]{1,0:T(8,128)} %param.30) | copy-start | bytes 20740
  77.4 286.2 %all-reduce.12.cloned.1.call-start = ((), (), s32[]{:S(2)}) async-start(), calls=%async_computation.10 | async-start | bytes 6291456
  93.3 166.9 %copy-start.54 = (s32[196]{0:T(256)}, s32[196]{0:T(256)S(1)}, u32[]{:S(2)}) copy-start(s32[196]{0:T(256)S(1)} %get-tuple-element.190) | copy-start | bytes 2356
  93.3 169.3 %copy-start.56 = (s32[196]{0:T(256)}, s32[196]{0:T(256)S(1)}, u32[]{:S(2)}) copy-start(s32[196]{0:T(256)S(1)} %get-tuple-element.189) | copy-start | bytes 2356
  93.4 68.8 %copy-start.42 = (s32[14,14]{1,0:T(8,128)}, s32[14,14]{1,0:T(8,128)S(1)}, u32[]{:S(2)}) copy-start(s32[14,14]{1,0:T(8,128)S(1)} %subtract_add_fusion) | copy-start | bytes 2356
  94.5 156.7 %copy-start.36 = (bf16[14,14,64,1,1]{2,1,4,3,0:T(8,128)(2,1)}, bf16[14,14,64,1,1]{2,1,4,3,0:T(8,128)(2,1)S(1)}, u32[]{:S(2)}) copy-start(bf16[14,14,64,1,1]{2,1,4,3,0:T(8,128)(2,1)S(1)} %fusion.34) | copy-start | bytes 75268
  182.9 68.2 %copy-start.3 = (bf16[9,14,14,3,64]{4,3,2,1,0:T(4,128)(2,1)}, bf16[9,14,14,3,64]{4,3,2,1,0:T(4,128)(2,1)S(1)}, u32[]{:S(2)}) copy-start(bf16[9,14,14,3,64]{4,3,2,1,0:T(4,128)(2,1)S(1)} %reshape.397) | copy-start | bytes 2032132
  232.0 36.6 %copy-start.7 = (bf16[9,196,3,64]{1,3,2,0:T(8,128)(2,1)}, bf16[9,196,3,64]{1,3,2,0:T(8,128)(2,1)S(1)}, u32[]{:S(2)}) copy-start(bf16[9,196,3,64]{1,3,2,0:T(8,128)(2,1)S(1)} %copy.116) | copy-start | bytes 2032132
  277.5 4.9 copy-start.20
  293.2 8.3 copy-start.69
  293.2 85.1 %all-gather.9.cloned.1.call-start = ((), (), s32[]{:S(2)}) async-start(), calls=%async_computation.2 | async-start | bytes 1769472 | tf_op jit(solution)/shard_map/all_gather | solution.py:269
  295.5 91.4 %all-gather.11.cloned.1.call-start = ((), (), s32[]{:S(2)}) async-start(), calls=%async_computation.4 | async-start | bytes 1769472 | tf_op jit(solution)/shard_map/all_gather | solution.py:270
  297.7 89.2 %all-gather.17.cloned.1.call-start = ((), (), s32[]{:S(2)}) async-start(), calls=%async_computation.7 | async-start | bytes 1966080 | tf_op jit(solution)/shard_map/all_gather | solution.py:228
  299.2 184.2 %reduce-scatter.5.cloned.1.call-start = ((), (), s32[]{:S(2)}) async-start(), calls=%async_computation.3 | async-start | bytes 15728640 | tf_op jit(solution)/shard_map/reduce_scatter | solution.py:309
  300.0 338.2 %copy-start.48 = (f32[192]{0:T(256)}, f32[192]{0:T(256)S(1)}, u32[]{:S(2)}) copy-start(f32[192]{0:T(256)S(1)} %dynamic_slice.90) | copy-start | bytes 2308
  300.8 85.3 %copy-start.50 = (f32[192]{0:T(256)}, f32[192]{0:T(256)S(1)}, u32[]{:S(2)}) copy-start(f32[192]{0:T(256)S(1)} %dynamic_slice.91) | copy-start | bytes 2308
  378.3 259.9 %copy-start.38 = (f32[1024]{0:T(1024)}, f32[1024]{0:T(1024)S(1)}, u32[]{:S(2)}) copy-start(f32[1024]{0:T(1024)S(1)} %get-tuple-element.178) | copy-start | bytes 12292
  386.1 191.4 %all-reduce.14.cloned.1.call-start = ((), (), s32[]{:S(2)}) async-start(), calls=%async_computation.11 | async-start | bytes 6291456
  483.3 12.4 %copy-start.17 = (f32[1024,768]{1,0:T(8,128)S(1)}, f32[1024,768]{1,0:T(8,128)}, u32[]{:S(2)}) copy-start(f32[1024,768]{1,0:T(8,128)} %reduce-scatter.5.cloned.1.call-done) | copy-start | bytes 9437188
  508.9 116.5 %copy-start.29 = (bf16[192,3072]{1,0:T(8,128)(2,1)S(1)}, bf16[192,3072]{1,0:T(8,128)(2,1)}, u32[]{:S(2)}) copy-start(bf16[192,3072]{1,0:T(8,128)(2,1)} %all-gather.9.cloned.1.call-done) | copy-start | bytes 3538948
  509.0 116.5 %all-gather.13.cloned.1.call-start = ((), (), s32[]{:S(2)}) async-start(), calls=%async_computation.5 | async-start | bytes 7864320 | tf_op jit(solution)/shard_map/all_gather | solution.py:323
  509.5 152.9 %all-gather.19.cloned.1.call-start = ((), (), s32[]{:S(2)}) async-start(), calls=%async_computation.8 | async-start | bytes 1966080 | tf_op jit(solution)/shard_map/all_gather | solution.py:228
  632.1 30.3 %copy-start.21 = (bf16[192,768]{1,0:T(8,128)(2,1)S(1)}, bf16[192,768]{1,0:T(8,128)(2,1)}, u32[]{:S(2)}) copy-start(bf16[192,768]{1,0:T(8,128)(2,1)} %all_gather.33) | copy-start | bytes 884740
  641.7 162.8 %all-gather.15.cloned.1.call-start = ((), (), s32[]{:S(2)}) async-start(), calls=%async_computation.6 | async-start | bytes 5898240 | tf_op jit(solution)/shard_map/all_gather | solution.py:228
  672.9 4.7 copy-start.8
  672.9 8.8 slice-start
  766.9 279.0 %all-reduce.16.cloned.1.call-start = ((), (), s32[]{:S(2)}) async-start(), calls=%async_computation.12 | async-start | bytes 14155776 | tf_op jit(solution)/shard_map/psum | solution.py:360
  771.2 6.4 copy-start.14
  771.3 6.3 copy-start.16
  771.3 33.3 %copy-start.13 = (bf16[1024,192]{0,1:T(8,128)(2,1)S(1)}, bf16[1024,192]{0,1:T(8,128)(2,1)}, u32[]{:S(2)}) copy-start(bf16[1024,192]{0,1:T(8,128)(2,1)} %copy-done.12) | copy-start | bytes 1179652
  813.3 8.2 copy-start.60
  813.3 8.4 copy-start.61
  813.3 8.6 copy-start.2
  821.4 5.6 copy-start.43
  821.9 5.4 copy-start.4
  827.0 5.9 copy-start.23
  827.4 7.5 copy-start.25
  836.9 54.9 %copy-start.19 = (f32[1024,192]{0,1:T(8,128)S(1)}, f32[1024,192]{0,1:T(8,128)}, u32[]{:S(2)}) copy-start(f32[1024,192]{0,1:T(8,128)} %get-tuple-element.168) | copy-start | bytes 2359300
  1045.9 9.3 copy-start.35
  (35 other events, 94.7 us)
Sparse Core Ops, SparseCore 0:
  77.5 79.6 reduce-scatter.6
  293.3 70.2 all-reduce.11
  509.1 68.4 all-reduce.13
  579.0 46.4 all-gather.12
  767.0 37.4 all-gather.14
Sparse Core Ops, SparseCore 1:
  295.8 22.9 all-gather.8
  320.7 22.6 all-gather.10
  345.4 26.2 all-gather.16
  386.2 97.1 reduce-scatter.4
  641.8 20.5 all-gather.18
  813.4 232.5 all-reduce.15
where the time goes:
time: 1070 us; the launch traced here: 1060 us
  waiting for transfers between devices  533 us (50%)
  local copies, waits for them, and re-layouts  257 us (24%)
  matrix products  118 us (11%)
  blocking collectives  102 us (10%)
  other arithmetic  31.3 us (3%)
  between operations  22.5 us (2%)
    unnamed x14, waiting for transfers between devices  191 us
    psum x1, waiting for transfers between devices, local(): lax.psum((grad_query, grad_key, grad_value, grad_out, grad_up, grad_down)...  153 us
    reduce_scatter x1, waiting for transfers between devices, local(): lax.psum_scatter(product(second_in, w_up), 'row', scatter_dimension=1, ti...  96.4 us
    unnamed x153, local copies, waits for them, and re-layouts  53.5 us
    all_gather x1, waiting for transfers between devices, local(): grad_pre_full = lax.all_gather(grad_pre, 'row', axis=1, tiled=True)  46.2 us
    all_gather x3, waiting for transfers between devices, gather_grads(): return lax.all_gather(stacked, 'row', axis=2, tiled=True)  46 us
    psum x1, blocking collectives, local(): lax.psum((spread_out(first_gain_grad, D, row_place), spread_out(first_shi...  45.1 us
    reshape x8, local copies, waits for them, and re-layouts, windowed(): return blocks.reshape(blocks.shape[0], WIN * WIN, head_count, HEAD_DIM)  28.6 us
  transfers between devices with their start and end apart: 11, of which 8 were waited for; matrix products, arithmetic and copies ran while one was open for 6% of the time, Pallas kernels for 0%

commit v1 on v0

v1 whole, which is shorter than its diff:
```python
import functools
import jax, jax.numpy as jnp
from jax import lax
from jax.sharding import PartitionSpec as P
from jax.experimental import pallas as pl
from jax.experimental.pallas import tpu as pltpu

WIN=14; SIDE=32; CELL=16; GRIDW=48; PAD=10; NEG=-1e30
SLOTS=((0,128),(128,128),(256,128),(384,64),(448,64),(512,64))
f32=jnp.float32; bf16=jnp.bfloat16

def nt(a,b): return lax.dot_general(a,b,(((1,),(1,)),((),())),preferred_element_type=f32)
def nn(a,b): return lax.dot_general(a,b,(((1,),(0,)),((),())),preferred_element_type=f32)
def tn(a,b): return lax.dot_general(a,b,(((0,),(0,)),((),())),preferred_element_type=f32)

def codes():
    i=jnp.arange(8*GRIDW,dtype=jnp.int32); cell=i%GRIDW; xx=cell%CELL
    cells=jnp.where(xx<WIN,(i//GRIDW)*1000+(cell//CELL)*WIN+xx,-100000)
    j=jnp.arange(8*SIDE,dtype=jnp.int32)
    toks=(j//SIDE)*1000+j%SIDE
    return cells,toks

def rel_operands(rel_h,rel_w):
    h=rel_h[::-1].astype(bf16).T; w=rel_w[::-1].astype(bf16).T
    z=jnp.zeros((2,128,256),bf16)
    n=2*WIN-1
    z=z.at[0,0:64,64:64+n].set(h).at[0,0:64,128+65:128+65+n].set(w)
    z=z.at[1,64:128,0:n].set(h).at[1,64:128,128+1:128+1+n].set(w)
    return z

def spot_to_cells(slot_ref,src,cells_col,toks_row,c0):
    pass

def place(z,feat,spots,dmat,g):
    for row,width,lane in spots:
        got=nt(dmat,feat[row:row+width,256*g:256*(g+1)]).astype(bf16)
        z[pl.ds(PAD+8*g,8),:,lane:lane+width]=got.reshape(8,GRIDW,width)

def head_consts():
    lane=lax.broadcasted_iota(jnp.int32,(WIN,CELL,128),2)
    y=lax.broadcasted_iota(jnp.int32,(WIN,CELL,128),0)
    x=lax.broadcasted_iota(jnp.int32,(WIN,CELL,128),1)
    return lane,y,x

def skew(t,sign):
    th=t[:,0:128]; tw=t[:,128:256]
    outs=[]; outw=[]
    for y in range(WIN):
        a=th[CELL*y:CELL*(y+1)]
        s=(sign*(y-13))%128
        outs.append(pltpu.roll(a,s,1) if s else a)
        if sign>0:
            outw.append(pltpu.roll(tw[CELL*y:CELL*(y+1)],0,1,stride=1,stride_axis=0))
    if sign<0:
        x=lax.broadcasted_iota(jnp.int32,(WIN*CELL,128),0)&(CELL-1)
        for bit in (1,2,4,8):
            tw=jnp.where((x&bit)>0,pltpu.roll(tw,128-bit,1),tw)
        outw=[tw]
    return jnp.concatenate(outs,0),jnp.concatenate(outw,0)

def query_operand(q,rel,base,lane2,own):
    t=nn(q,rel)
    a,b=skew(t,1)
    in_h=(lane2>=base)&(lane2<base+WIN); in_w=(lane2>=base+WIN)&(lane2<base+2*WIN)
    both=jnp.where(in_h,a,jnp.where(in_w,b,0.0))
    hi=both.astype(bf16)
    lo=(both-hi.astype(f32)).astype(bf16)
    one=(lane2==base+2*WIN).astype(f32)
    first=(q.astype(f32)*0.125+hi.astype(f32)+one).astype(bf16)
    return jnp.concatenate([first,lo],1)

def key_operand(k,base,wy,wx,r0,c0):
    lane,y,x=head_consts()
    g=WIN*wy+y-r0; c=WIN*wx+x-c0
    ok=(g>=0)&(g<SIDE)&(c>=0)&(c<SIDE)&(x<WIN)
    eye=(((lane-base)==y)|((lane-base-WIN)==x)&(x<WIN)).astype(f32)
    eye=eye.reshape(WIN*CELL,128)
    mask=jnp.where((lane==base+2*WIN)&jnp.logical_not(ok),NEG,0.0).reshape(WIN*CELL,128)
    first=(k.astype(f32)+eye+mask).astype(bf16)
    return jnp.concatenate([first,eye.astype(bf16)],1)

HEADS3=((0,128*0,0),(1,128*0,0),(0,128*3,1))

def load_win(z,wy,wx,r0,lane):
    row=WIN*wy-r0+PAD
    return z[pl.ds(row,WIN),pl.ds(pl.multiple_of(CELL*wx,CELL),CELL),lane:lane+128].reshape(WIN*CELL,128)

def half_mask(v,half,lane2):
    keep=(lane2<64) if half==0 else (lane2>=64)
    return jnp.where(keep,v.astype(f32),0.0).astype(bf16)

def fwd_kernel(off,qkv,rel,cells,toks,o_ref,z,ow):
    r0=off[0,0]; c0=off[0,1]
    dmat=((cells[...]-c0)==toks[...]).astype(f32).astype(bf16)
    z[0:PAD]=jnp.zeros((PAD,GRIDW,768),bf16)
    z[PAD+SIDE:]=jnp.zeros((PAD,GRIDW,768),bf16)
    for lane in (384,512,640):
        z[PAD:PAD+SIDE,:,lane:lane+128]=jnp.zeros((SIDE,GRIDW,128),bf16)
    spots=[(r,w,128*i) for i,(r,w) in enumerate(SLOTS)]
    for g in range(4): place(z,qkv,spots,dmat,g)
    def window(n,carry):
        wy=n//3; wx=n%3
        lane2=lax.broadcasted_iota(jnp.int32,(WIN*CELL,128),1)
        for pair in range(2):
            q=load_win(z,wy,wx,r0,384*pair); k=load_win(z,wy,wx,r0,384*pair+128); v=load_win(z,wy,wx,r0,384*pair+256)
            total=None
            for half in range(2-pair):
                base=64 if half==0 else 0
                qq=half_mask(q,half,lane2); kk=half_mask(k,half,lane2)
                qc=query_operand(qq,rel[half],base,lane2,half)
                kc=key_operand(kk,base,wy,wx,r0,c0)
                s=nt(qc,kc)
                m=jnp.max(s,axis=1,keepdims=True)
                e=jnp.exp(s-m)
                p=(e*(1.0/jnp.sum(e,axis=1,keepdims=True))).astype(bf16)
                o=nn(p,v)
                total=o if total is None else jnp.where(lane2<64,total,o)
            ow[pl.ds(WIN*wy,WIN),pl.ds(pl.multiple_of(CELL*wx,CELL),CELL),128*pair:128*pair+128]=total.astype(bf16).reshape(WIN,CELL,128)
        return carry
    lax.fori_loop(0,9,window,0)
    for g in range(4):
        rows=ow[pl.ds(r0+8*g,8)].reshape(8*GRIDW,256)
        got=tn(dmat,rows)
        o_ref[256*g:256*(g+1),0:192]=got[:,0:192].astype(bf16)

def attend(off,qkv,rel):
    cells,toks=codes()
    return pl.pallas_call(fwd_kernel,out_shape=jax.ShapeDtypeStruct((1024,192),bf16),
      in_specs=[pl.BlockSpec(memory_space=pltpu.SMEM)]+[pl.BlockSpec(memory_space=pltpu.VMEM)]*4,
      out_specs=pl.BlockSpec(memory_space=pltpu.VMEM),
      scratch_shapes=[pltpu.VMEM((SIDE+2*PAD,GRIDW,768),bf16),pltpu.VMEM((42,GRIDW,256),bf16)],
      compiler_params=pltpu.CompilerParams(vmem_limit_bytes=56<<20),name="attend",
    )(off,qkv,rel,cells[:,None],toks[None,:])

def bwd_kernel(off,qkv,do,rel,cells,toks,g_ref,drel_ref,z,gw,tw):
    r0=off[0,0]; c0=off[0,1]
    dmat=((cells[...]-c0)==toks[...]).astype(f32).astype(bf16)
    z[0:PAD]=jnp.zeros((PAD,GRIDW,1024),bf16)
    z[PAD+SIDE:]=jnp.zeros((PAD,GRIDW,1024),bf16)
    for lane in (384,512,640,896):
        z[PAD:PAD+SIDE,:,lane:lane+128]=jnp.zeros((SIDE,GRIDW,128),bf16)
    spots=[(r,w,128*i) for i,(r,w) in enumerate(SLOTS)]
    for g in range(4):
        place(z,qkv,spots,dmat,g)
        place(z,do,((0,128,768),(128,64,896)),dmat,g)
    drel_ref[...]=jnp.zeros(drel_ref.shape,f32)
    def window(n,carry):
        wy=n//3; wx=n%3
        lane2=lax.broadcasted_iota(jnp.int32,(WIN*CELL,128),1)
        lane4=lax.broadcasted_iota(jnp.int32,(WIN*CELL,256),1)
        for pair in range(2):
            q=load_win(z,wy,wx,r0,384*pair); k=load_win(z,wy,wx,r0,384*pair+128); v=load_win(z,wy,wx,r0,384*pair+256)
            d=load_win(z,wy,wx,r0,768+128*pair)
            dq=dk=dv=None
            for half in range(2-pair):
                base=64 if half==0 else 0
                qq=half_mask(q,half,lane2); kk=half_mask(k,half,lane2); dd=half_mask(d,half,lane2)
                qc=query_operand(qq,rel[half],base,lane2,half)
                kc=key_operand(kk,base,wy,wx,r0,c0)
                s=nt(qc,kc)
                m=jnp.max(s,axis=1,keepdims=True)
                e=jnp.exp(s-m)
                p=e*(1.0/jnp.sum(e,axis=1,keepdims=True))
                pb=p.astype(bf16)
                dp=nt(dd,v)
                centre=jnp.sum(p*dp,axis=1,keepdims=True)
                ds=(p*(dp-centre)).astype(bf16)
                dvh=tn(pb,dd)
                dkh=tn(ds,qq)*0.125
                dqc=nn(ds,kc[:,0:128])
                t=jnp.concatenate([jnp.where((lane2>=base)&(lane2<base+WIN),dqc,0.0),
                                   jnp.where((lane2>=base+WIN)&(lane2<base+2*WIN),dqc,0.0)],1)
                a,b=skew(t,-1)
                t=jnp.concatenate([a,b],1)
                thi=t.astype(bf16)
                tlo=(t-thi.astype(f32)).astype(bf16)
                own=(lane2<64) if half==0 else (lane2>=64)
                dqh=jnp.where(own,dqc*0.125,0.0)+nt(thi,rel[half])+nt(tlo,rel[half])
                drel_ref[half]+=tn(qq,thi)
                if dq is None: dq,dk,dv=dqh,dkh,dvh
                else: dq,dk,dv=dq+dqh,dk+dkh,dv+dvh
            rows=pl.ds(WIN*wy,WIN); cols=pl.ds(pl.multiple_of(CELL*wx,CELL),CELL)
            for i,val in enumerate((dq,dk,dv)):
                lane=384*pair+128*i
                gw[rows,cols,lane:lane+128]=val.astype(bf16).reshape(WIN,CELL,128)
        return carry
    lax.fori_loop(0,9,window,0)
    for g in range(4):
        for i,(r,w) in enumerate(SLOTS):
            rows=gw[pl.ds(r0+8*g,8),:,128*i:128*i+128].reshape(8*GRIDW,128)
            got=tn(dmat,rows)
            g_ref[256*g:256*(g+1),r:r+w]=got[:,0:w].astype(bf16)

def attend_back(off,qkv,do,rel):
    cells,toks=codes()
    return pl.pallas_call(bwd_kernel,out_shape=(jax.ShapeDtypeStruct((1024,576),bf16),jax.ShapeDtypeStruct((2,128,256),f32)),
      in_specs=[pl.BlockSpec(memory_space=pltpu.SMEM)]+[pl.BlockSpec(memory_space=pltpu.VMEM)]*5,
      out_specs=(pl.BlockSpec(memory_space=pltpu.VMEM),)*2,
      scratch_shapes=[pltpu.VMEM((SIDE+2*PAD,GRIDW,1024),bf16),pltpu.VMEM((42,GRIDW,768),bf16),pltpu.VMEM((8,128),f32)],
      compiler_params=pltpu.CompilerParams(vmem_limit_bytes=56<<20),name="attend_back",
    )(off,qkv,do,rel,cells[:,None],toks[None,:])

def rel_grads(drel):
    n=2*WIN-1
    h=drel[0,0:64,64:64+n]+drel[1,64:128,0:n]
    w=drel[0,0:64,193:193+n]+drel[1,64:128,129:129+n]
    return h.T[::-1],w.T[::-1]

EPS=1e-06
D=768

def gelu_parts(h):
    cdf=0.5*(1.0+lax.erf(h*0.7071067811865476))
    pdf=jnp.exp(-0.5*h*h)*0.3989422804014327
    return h*cdf,cdf+h*pdf

def own_rows(vector,length,place):
    return lax.dynamic_slice_in_dim(vector,place*length,length,0)

def spread(portion,whole,place):
    return lax.dynamic_update_slice_in_dim(jnp.zeros((whole,),f32),portion,place*portion.shape[0],0)

def head_order(q,k,v):
    return jnp.concatenate([q[...,0:128],k[...,0:128],v[...,0:128],q[...,128:],k[...,128:],v[...,128:]],-1)

def head_unorder(m):
    cat=lambda a,b:jnp.concatenate([m[...,a:a+128],m[...,b:b+64]],-1)
    return cat(0,384),cat(128,448),cat(256,512)

def gather_rows(block):
    return lax.all_gather(block,"row",axis=0,tiled=True)

def sum_rows(partial):
    return lax.psum_scatter(partial.astype(bf16),"row",scatter_dimension=0,tiled=True).astype(f32)

def row_stats(*vals):
    both=lax.psum(jnp.stack([jnp.sum(v,axis=0) for v in vals]),"row")
    return [both[i:i+1]/D for i in range(len(vals))]

def local(tokens,cotangent,offsets,ln1_gain,ln1_bias,q_weight,k_weight,v_weight,q_bias,v_bias,rel_pos_h,rel_pos_w,
          out_weight,out_bias,ln2_gain,ln2_bias,up_weight,up_bias,down_weight,down_bias):
    rows=lax.axis_size("row"); r=lax.axis_index("row"); cols=lax.axis_size("col")
    width=tokens.shape[0]; hidden=up_bias.shape[0]//rows
    gather_col=lambda w:lax.all_gather(w.astype(bf16),"col",axis=1,tiled=True)
    per=rows//cols
    def quarters(w):
        n=w.shape[1]//per
        return [w[:,n*i:n*i+n].astype(bf16) for i in range(per)]
    qs=[head_order(a,b,c) for a,b,c in zip(quarters(q_weight),quarters(k_weight),quarters(v_weight))]
    us=quarters(up_weight)
    own=jnp.stack([jnp.concatenate([a,b],1) for a,b in zip(qs,us)],1)
    full=lax.all_gather(own,"col",axis=1,tiled=True)
    turned=lax.all_to_all(full,"row",split_axis=1,concat_axis=0,tiled=True).reshape(D,-1)
    w_qkv=turned[:,0:576]; w_up=turned[:,576:]
    w_out=gather_col(out_weight); w_down=gather_col(down_weight)
    col=lambda vec,n:own_rows(vec,n,r)[:,None]
    g1,s1,g2,s2=[col(v,width) for v in (ln1_gain,ln1_bias,ln2_gain,ln2_bias)]
    bq=own_rows(q_bias,width,r); bv=own_rows(v_bias,width,r)
    b_qkv=head_order(bq,jnp.zeros_like(bq),bv)[:,None]
    b_out,b_down=col(out_bias,width),col(down_bias,width); b_up=col(up_bias,hidden)
    rel=rel_operands(rel_pos_h,rel_pos_w)
    x=tokens
    m,sq=row_stats(x,x*x)
    inv1=lax.rsqrt(sq-m*m+EPS); norm1=(x-m)*inv1
    a1=gather_rows((norm1*g1+s1).astype(bf16))
    qkv=(tn(w_qkv,a1)+b_qkv).astype(bf16)
    o=attend(offsets,qkv,rel)
    x1=x+sum_rows(lax.dot_general(w_out,o,(((0,),(1,)),((),())),preferred_element_type=f32))+b_out
    m2,sq2=row_stats(x1,x1*x1)
    inv2=lax.rsqrt(sq2-m2*m2+EPS); norm2=(x1-m2)*inv2
    a2=gather_rows((norm2*g2+s2).astype(bf16))
    h=tn(w_up,a2)+b_up
    act,slope=gelu_parts(h)
    g=act.astype(bf16)
    output=x1+sum_rows(tn(w_down,g))+b_down
    dy_own=cotangent.astype(bf16)
    dy=gather_rows(dy_own)
    d_down_bias=jnp.sum(dy_own,axis=1,dtype=f32)
    dh=(nn(w_down,dy)*slope).astype(bf16)
    d_down=nt(g,dy).astype(bf16)
    d_up=nt(a2,dh).astype(bf16)
    d_up_bias=jnp.sum(dh,axis=1,dtype=f32)
    da2=sum_rows(nn(w_up,dh))
    d_g2=jnp.sum(da2*norm2,axis=1); d_s2=jnp.sum(da2,axis=1)
    e2=da2*g2
    u,w=row_stats(e2,e2*norm2)
    dx1=cotangent+inv2*(e2-u-norm2*w)
    dat_own=dx1.astype(bf16)
    d_out_bias=jnp.sum(dat_own,axis=1,dtype=f32)
    dat=gather_rows(dat_own)
    d_out=lax.dot_general(o,dat,(((0,),(1,)),((),())),preferred_element_type=f32).astype(bf16)
    do=nn(w_out,dat).astype(bf16)
    dqkv,drel=attend_back(offsets,qkv,do,rel)
    d_qkv=nn(a1,dqkv).astype(bf16)
    b_sums=head_unorder(jnp.sum(dqkv,axis=0,dtype=f32))
    da1=sum_rows(nt(w_qkv,dqkv))
    d_g1=jnp.sum(da1*norm1,axis=1); d_s1=jnp.sum(da1,axis=1)
    e1=da1*g1
    u,w=row_stats(e1,e1*norm1)
    input_grad=dx1+inv1*(e1-u-norm1*w)
    def turn_back(dw):
        n=dw.shape[1]
        t=lax.all_to_all(dw.reshape(rows,width,n),"row",split_axis=0,concat_axis=0,tiled=True)
        return t
    def reduce(t,axis):
        return lax.psum(lax.psum_scatter(t,"col",scatter_dimension=axis,tiled=True),"dp").astype(f32)
    t_up=reduce(turn_back(d_up),0); t_qkv=reduce(turn_back(d_qkv),0)
    f_up=jnp.concatenate([t_up[i] for i in range(per)],1)
    parts=[head_unorder(t_qkv[i]) for i in range(per)]
    f_q,f_k,f_v=[jnp.concatenate([p[i] for p in parts],1) for i in range(3)]
    f_down=reduce(d_down,1); f_out=reduce(d_out,1)
    dh_rel,dw_rel=rel_grads(drel)
    minor=lax.psum((spread(d_g1,D,r),spread(d_s1,D,r),spread(b_sums[0],D,r),spread(b_sums[2],D,r),dh_rel,dw_rel,
      spread(d_out_bias,D,r),spread(d_g2,D,r),spread(d_s2,D,r),spread(d_up_bias,up_bias.shape[0],r),spread(d_down_bias,D,r)),("dp","row","col"))
    return (output,input_grad,minor[0],minor[1],f_q,f_k,f_v,minor[2],minor[3],minor[4],minor[5],f_out,minor[6],minor[7],
            minor[8],f_up,minor[9],f_down,minor[10])

def solution(mesh):
    act=P("row",("dp","col")); mat=P("row","col"); rep=P()
    return jax.shard_map(local,mesh=mesh,
      in_specs=(act,act,P(("dp","col"),None),rep,rep,mat,mat,mat,rep,rep,rep,rep,mat,rep,rep,rep,mat,rep,mat,rep),
      out_specs=(act,act,rep,rep,mat,mat,mat,rep,rep,rep,rep,mat,rep,rep,rep,mat,rep,mat,rep),check_vma=False)
```

time: 1070 us -> 548 us (0.51)
  waiting for transfers between devices: 533 us -> 258 us
  local copies, waits for them, and re-layouts: 257 us -> 32.8 us
  matrix products: 118 us -> 46 us
  Pallas kernels: 0 us -> 58.5 us
    unnamed x14 -> x17, waiting for transfers between devices: 191 us -> 0.25 us
    psum x1, waiting for transfers between devices: 153 us -> 56.8 us  [reduce(): lax.psum(lax.psum_scatter(t, 'col', scatter_dimension=axis, tiled=True),...]
    reshape x29 -> x0, local copies, waits for them, and re-layouts: 92.6 us -> none  [the longest x8 28.6 us: windowed(): return blocks.reshape(blocks.shape[0], WIN * WIN, head_count, HEAD_DIM)]
    dot_general x38 -> x12, matrix products: 118 us -> 46 us  [the longest x4 15.6 us: nn(): lax.dot_general(a, b, (((1,), (0,)), ((), ())), preferred_element_type=f32)]
    pallas_call x0 -> x2, Pallas kernels: none -> 58.5 us  [the longest x1 41.2 us: attend_back(): pl.pallas_call(bwd_kernel, out_shape=(jax.ShapeDtypeStruct((1024, 576), b...]
    unnamed x153 -> x78, local copies, waits for them, and re-layouts: 53.5 us -> 18.6 us
    transpose x12 -> x0, local copies, waits for them, and re-layouts: 29.7 us -> none  [the longest x4 7.88 us: to_windows(): padded.reshape(blocks_side, WIN, blocks_side, WIN, channels)]
    all_gather x4 -> x1, blocking collectives: 25.6 us -> 6.81 us  [local(): lax.all_gather(w.astype(bf16), 'col', axis=1, tiled=True)]
  transfers between devices with their start and end apart: 11 -> 17, of which waited for: 8 -> 13; matrix products, arithmetic and copies ran while one was open for 6% -> 12% of each run, Pallas kernels for 0% -> 8%
where the time goes in v1:
time: 548 us; the launch traced here: 540 us
  waiting for transfers between devices  258 us (47%)
  blocking collectives  92.7 us (17%)
  Pallas kernels  58.5 us (11%)
  matrix products  46 us (8%)
  local copies, waits for them, and re-layouts  32.8 us (6%)
  other arithmetic  27.7 us (5%)
  between operations  15 us (3%)
  starting transfers between devices  9.24 us (2%)
    reduce_scatter x4, waiting for transfers between devices, sum_rows(): lax.psum_scatter(partial.astype(bf16), 'row', scatter_dimension=0, tiled=...  81.4 us
    all_gather x4, waiting for transfers between devices, gather_rows(): return lax.all_gather(block, 'row', axis=0, tiled=True)  61.8 us
    psum x1, waiting for transfers between devices, reduce(): lax.psum(lax.psum_scatter(t, 'col', scatter_dimension=axis, tiled=True),...  56.8 us
    psum x1, blocking collectives, local(): lax.psum((spread(d_g1, D, r), spread(d_s1, D, r), spread(b_sums[0], D, r)...  41.7 us
    pallas_call x1, Pallas kernels, attend_back(): pl.pallas_call(bwd_kernel, out_shape=(jax.ShapeDtypeStruct((1024, 576), b...  41.2 us
    psum x4, blocking collectives, row_stats(): both = lax.psum(jnp.stack([jnp.sum(v, axis=0) for v in vals]), 'row')  27.4 us
    all_gather x1, waiting for transfers between devices, local(): full = lax.all_gather(own, 'col', axis=1, tiled=True)  25.4 us
    all_gather x1, waiting for transfers between devices, local(): lax.all_gather(w.astype(bf16), 'col', axis=1, tiled=True)  18.8 us
  transfers between devices with their start and end apart: 17, of which 13 were waited for; matrix products, arithmetic and copies ran while one was open for 12% of the time, Pallas kernels for 8%

profile of v1, /device:TPU:0, one launch (start us, length us, event | category | flops | bytes accessed | tf_op | source)
XLA Modules:
  0.0 540.0 jit_solution(13138001527596107814)
XLA Ops:
  13.7 8.5 %psum.133 = f32[2,1024]{1,0:T(2,128)S(1)} all-reduce(f32[2,1024]{1,0:T(2,128)S(1)} %pad_maximum_fusion.5), channel_id=1, replica_groups=mesh['dp'=4,'row'=4,'col'=2] {'row'}, use_global_device_ids=true, to_apply=%region_2.0 | all-reduce | flops 2048 | bytes 16384 | tf_op jit(solution)/shard_map/psum | solution.py:237
  23.3 25.4 %all-gather.7.cloned.1.call-done = bf16[192,4,1344]{2,0,1:T(8,128)(2,1)} async-done(((bf16[192,2,1344]{2,0,1:T(8,128)(2,1)}), bf16[192,4,1344]{2,0,1:T(8,128)(2,1)}) %all-gather.7.cloned.1.call-update) | async-done | bytes 2064400 | tf_op jit(solution)/shard_map/all_gather | solution.py:252
  48.7 4.5 all-to-all-start
  57.3 6.8 %all_gather.23 = bf16[192,768]{1,0:T(8,128)(2,1)S(1)} all-gather(bf16[192,384]{1,0:T(8,128)(2,1)S(1)} %convert_element_type.116), channel_id=1, replica_groups=mesh['dp'=4,'row'=4,'col'=2] {'col'}, dimensions={1}, use_global_device_ids=true | all-gather | bytes 442368 | tf_op jit(solution)/shard_map/all_gather | solution.py:244
  65.7 13.3 %all-gather.9.cloned.1.call-done = bf16[768,1024]{1,0:T(8,128)(2,1)} async-done(((bf16[192,1024]{1,0:T(8,128)(2,1)}), bf16[768,1024]{1,0:T(8,128)(2,1)}) %all-gather.9.cloned.1.call-update) | async-done | bytes 1572880 | tf_op jit(solution)/shard_map/all_gather | solution.py:231
  79.0 9.0 %all-to-all-done = bf16[192,4,1344]{2,0,1:T(8,128)(2,1)} async-done(((bf16[192,4,1344]{2,0,1:T(8,128)(2,1)}), bf16[192,4,1344]{2,0,1:T(8,128)(2,1)}, u32[]{:S(2)}, u32[]{:S(2)}) %all-to-all-start) | async-done | bytes 2064416 | tf_op jit(solution)/shard_map/all_to_all | solution.py:253
  88.0 3.8 add_convert_fusion.qkv
  91.8 17.3 %attend.1 = bf16[1024,192]{1,0:T(8,128)(2,1)} custom-call(s32[1,2]{1,0:T(1,128)} %off.3, bf16[576,1024]{1,0:T(8,128)(2,1)} %add_convert_fusion.qkv, bf16[2,128,256]{2,1,0:T(8,128)(2,1)} %copy-done.8, s32[384,1]{1,0:T(8,128)} %fusion.39.cells, s32[1,256]{1,0:T(1,128)} %fusion.49.toks), custom_call_target="tpu_custom_call" | custom-call | tf_op jit(solution)/shard_map/attend/pallas_call | solution.py:128
  109.2 1.6 fusion.6
  110.8 1.7 copy.74
  114.8 24.9 %reduce-scatter.25.cloned.1.call-done = bf16[192,1024]{1,0:T(8,128)(2,1)} async-done(((bf16[768,1024]{1,0:T(8,128)(2,1)}), bf16[192,1024]{1,0:T(8,128)(2,1)}) %reduce-scatter.25.cloned.1.call-update) | async-done | bytes 393232 | tf_op jit(solution)/shard_map/reduce_scatter | solution.py:234
  140.9 5.9 %psum.134 = f32[2,1024]{1,0:T(2,128)S(1)} all-reduce(f32[2,1024]{1,0:T(2,128)S(1)} %pad_maximum_fusion.6), channel_id=1, replica_groups=mesh['dp'=4,'row'=4,'col'=2] {'row'}, use_global_device_ids=true, to_apply=%region_6.0 | all-reduce | flops 2048 | bytes 16384 | tf_op jit(solution)/shard_map/psum | solution.py:237
  151.5 16.8 %all-gather.11.cloned.1.call-done = bf16[768,1024]{1,0:T(8,128)(2,1)} async-done(((bf16[192,1024]{1,0:T(8,128)(2,1)}), bf16[768,1024]{1,0:T(8,128)(2,1)}) %all-gather.11.cloned.1.call-update) | async-done | bytes 1572880 | tf_op jit(solution)/shard_map/all_gather | solution.py:231
  168.2 6.0 %multiply_convert_fusion = (bf16[768,1024]{1,0:T(8,128)(2,1)}, f32[768,1024]{1,0:T(8,128)}) fusion(f32[768]{0:T(1024)S(1)} %dynamic_slice.34, bf16[768,1024]{1,0:T(8,128)(2,1)} %all-gather.11.cloned.1.call-done, bf16[768,1344]{1,0:T(8,128)(2,1)} %bitcast.4), kind=kOutput, calls=%fused_computation.8 | convolution fusion | flops 1212678144 | bytes 7474176 | tf_op jit(solution)/shard_map/dot_general | solution.py:14
  174.2 18.8 %all-gather.13.cloned.1.call-done = bf16[768,768]{1,0:T(8,128)(2,1)} async-done(((bf16[768,384]{1,0:T(8,128)(2,1)}), bf16[768,768]{1,0:T(8,128)(2,1)}) %all-gather.13.cloned.1.call-update) | async-done | bytes 1179664 | tf_op jit(solution)/shard_map/all_gather | solution.py:244
  193.0 21.1 %all-gather.15.cloned.1.call-done = bf16[768,1024]{1,0:T(8,128)(2,1)} async-done(((bf16[192,1024]{1,0:T(8,128)(2,1)}), bf16[768,1024]{1,0:T(8,128)(2,1)}) %all-gather.15.cloned.1.call-update) | async-done | bytes 1572880 | tf_op jit(solution)/shard_map/all_gather | solution.py:231
  214.0 5.4 %convert_reduce_fusion = (f32[768]{0:T(1024)}, bf16[768,1024]{1,0:T(8,128)(2,1)S(1)}) fusion(f32[768,1024]{1,0:T(8,128)} %get-tuple-element.207, f32[768]{0:T(1024)S(1)} %dynamic_slice.34, bf16[768,768]{1,0:T(8,128)(2,1)} %all-gather.13.cloned.1.call-done, bf16[768,1024]{1,0:T(8,128)(2,1)} %all-gather.15.cloned.1.call-done), kind=kOutput, calls=%fused_computation.7 | convolution fusion | flops 1218182400 | bytes 7477248 | tf_op jit(solution)/shard_map/dot_general | solution.py:13
  220.7 3.9 convolution_convert_fusion.1
  224.7 28.1 %reduce-scatter.29.cloned.1.call-done = bf16[192,1024]{1,0:T(8,128)(2,1)} async-done(((bf16[768,1024]{1,0:T(8,128)(2,1)}), bf16[192,1024]{1,0:T(8,128)(2,1)}) %reduce-scatter.29.cloned.1.call-update) | async-done | bytes 393232 | tf_op jit(solution)/shard_map/reduce_scatter | solution.py:234
  252.8 1.9 fusion.28
  254.7 5.9 %psum.135 = f32[2,1024]{1,0:T(2,128)S(1)} all-reduce(f32[2,1024]{1,0:T(2,128)S(1)} %pad_maximum_fusion.7), channel_id=1, replica_groups=mesh['dp'=4,'row'=4,'col'=2] {'row'}, use_global_device_ids=true, to_apply=%region_11.12 | all-reduce | flops 2048 | bytes 16384 | tf_op jit(solution)/shard_map/psum | solution.py:237
  260.7 2.7 convert_reduce_fusion.5
  263.4 3.3 convolution_convert_fusion.4
  266.7 1.5 copy.84
  268.2 4.4 convolution_convert_fusion.5
  272.6 3.5 all-to-all-start.2
  276.2 10.7 %all-gather.17.cloned.1.call-done = bf16[768,1024]{1,0:T(8,128)(2,1)} async-done(((bf16[192,1024]{1,0:T(8,128)(2,1)}), bf16[768,1024]{1,0:T(8,128)(2,1)}) %all-gather.17.cloned.1.call-update) | async-done | bytes 1572880 | tf_op jit(solution)/shard_map/all_gather | solution.py:231
  286.8 3.0 convolution_convert_fusion.8
  289.8 1.9 copy.82
  291.7 3.2 all-to-all-done.2
  296.2 2.8 fusion.8.do
  299.0 41.2 %attend_back.1 = (bf16[1024,576]{1,0:T(8,128)(2,1)}, f32[2,128,256]{2,1,0:T(8,128)}) custom-call(s32[1,2]{1,0:T(1,128)} %off.3, bf16[576,1024]{1,0:T(8,128)(2,1)} %add_convert_fusion.qkv, bf16[192,1024]{1,0:T(8,128)(2,1)} %fusion.8.do, bf16[2,128,256]{2,1,0:T(8,128)(2,1)} %copy-done.8, s32[384,1]{1,0:T(8,128)} %fusion.39.cells, s32[1,256]{1,0:T(1,128)} %fusion.49.toks), custom_call_target="tpu_custom_call" | custom-call | tf_op jit(solution)/shard_map/attend_back/pallas_call | solution.py:196
  340.3 3.4 convolution_convert_fusion.6
  343.6 1.5 copy.71
  345.2 16.9 %all_to_all.25 = bf16[4,192,576]{2,1,0:T(8,128)(2,1)} all-to-all(bf16[4,192,576]{2,1,0:T(8,128)(2,1)S(1)} %bitcast.86), channel_id=1, replica_groups=mesh['dp'=4,'row'=4,'col'=2] {'row'}, dimensions={0} | all-to-all | bytes 1769472 | tf_op jit(solution)/shard_map/all_to_all | solution.py:303
  362.1 4.2 convolution_convert_fusion
  367.5 4.2 fusion.7
  371.7 2.6 copy.76
  375.9 2.2 copy.85
  378.8 1.7 copy.83
  380.5 1.4 reduce-scatter.21.cloned.1.call-done
  382.2 1.6 convert_reduce_fusion.1
  384.0 28.4 %reduce-scatter.31.cloned.1.call-done = bf16[192,1024]{1,0:T(8,128)(2,1)} async-done(((bf16[768,1024]{1,0:T(8,128)(2,1)}), bf16[192,1024]{1,0:T(8,128)(2,1)}) %reduce-scatter.31.cloned.1.call-update) | async-done | bytes 393232 | tf_op jit(solution)/shard_map/reduce_scatter | solution.py:234
  412.4 1.4 fusion.29
  414.4 41.7 %all-reduce.1 = (f32[768]{0:T(1024)}, f32[768]{0:T(1024)}, f32[768]{0:T(1024)}, f32[768]{0:T(1024)}, f32[27,64]{0,1:T(8,128)S(1)}, /*index=5*/f32[27,64]{0,1:T(8...) all-reduce(f32[768]{0:T(1024)S(1)} %dynamic_update_slice.27, ...), channel_id=1, replica_groups=mesh['dp'=4,'row'=4,'col'=2] {'dp','row','col'}, use_global_device_ids=true, to_apply=%region_17.18 | all-reduce | flops 12672 | bytes 101376 | tf_op jit(solution)/shard_map/psum | solution.py:313
  457.4 7.1 %psum.136 = f32[2,1024]{1,0:T(2,128)S(1)} all-reduce(f32[2,1024]{1,0:T(2,128)S(1)} %pad_maximum_fusion.8), channel_id=1, replica_groups=mesh['dp'=4,'row'=4,'col'=2] {'row'}, use_global_device_ids=true, to_apply=%region_15.16 | all-reduce | flops 2048 | bytes 16384 | tf_op jit(solution)/shard_map/psum | solution.py:237
  464.6 2.7 fusion.23
  467.3 56.8 %all-reduce.5.cloned.1.call-done = (bf16[2,192,576]{2,1,0:T(8,128)(2,1)}, bf16[192,384]{1,0:T(8,128)(2,1)}, bf16[2,192,768]{2,1,0:T(8,128)(2,1)}, bf16[768,384]{1,0:T(8,128)(2,1)}) async-done(((bf16[2,192,576]{2,1,0:T(8,128)(2,1)}, bf16[192,384]{1,0:T(8,128)(2,1)}, bf16[2,192,768]{2,1,0:T(8,128)(2,1)}, bf16[768,384]{1,0:T(8,128)(2,1)}), (bf16[2,192,576]{2,1,0:T(8,128)(2,1)}, bf16[192,384]{1,0:T(8,128)(2,1)}, ...) | async-done | bytes 1769488 | tf_op jit(solution)/shard_map/psum | solution.py:306
  (194 shorter events, 38.7 us)
Async XLA Ops:
  7.2 2.3 copy-start.11
  7.2 2.5 copy-start.6
  7.2 41.5 %all-gather.7.cloned.1.call-start = ((), (), s32[]{:S(2)}) async-start(), calls=%async_computation.11 | async-start | bytes 3244032 | tf_op jit(solution)/shard_map/all_gather | solution.py:252
  10.8 2.7 copy-start
  12.0 67.0 %all-gather.9.cloned.1.call-start = ((), (), s32[]{:S(2)}) async-start(), calls=%async_computation.12 | async-start | bytes 1966080 | tf_op jit(solution)/shard_map/all_gather | solution.py:231
  12.8 10.4 %copy-start.24 = (f32[192]{0:T(256)}, f32[192]{0:T(256)S(1)}, u32[]{:S(2)}) copy-start(f32[192]{0:T(256)S(1)} %dynamic_slice.27) | copy-start | bytes 2308
  23.2 31.5 %copy-start.22 = (f32[27,64]{1,0:T(8,128)S(1)}, f32[27,64]{1,0:T(8,128)}, u32[]{:S(2)}) copy-start(f32[27,64]{1,0:T(8,128)} %param.38) | copy-start | bytes 20740
  23.2 31.7 %copy-start.23 = (f32[27,64]{1,0:T(8,128)S(1)}, f32[27,64]{1,0:T(8,128)}, u32[]{:S(2)}) copy-start(f32[27,64]{1,0:T(8,128)} %param.39) | copy-start | bytes 20740
  23.2 31.9 %copy-start.12 = (f32[192,384]{1,0:T(8,128)S(1)}, f32[192,384]{1,0:T(8,128)}, u32[]{:S(2)}) copy-start(f32[192,384]{1,0:T(8,128)} %param.40) | copy-start | bytes 884740
  48.7 39.3 %all-to-all-start = ((bf16[192,4,1344]{2,0,1:T(8,128)(2,1)}), bf16[192,4,1344]{2,0,1:T(8,128)(2,1)}, u32[]{:S(2)}, u32[]{:S(2)}) async-start(bf16[192,4,1344]{2,0,1:T(8,128)(2,1)} %all-gather.7.cloned.1.call-done), calls=%async_computation | async-start | bytes 4325376 | tf_op jit(solution)/shard_map/all_to_all | solution.py:253
  53.1 86.6 %reduce-scatter.25.cloned.1.call-start = ((), (), s32[]{:S(2)}) async-start(), calls=%async_computation.19 | async-start | bytes 1966080 | tf_op jit(solution)/shard_map/reduce_scatter | solution.py:234
  57.2 34.7 %copy-start.8 = (bf16[2,128,256]{2,1,0:T(8,128)(2,1)}, bf16[2,128,256]{2,1,0:T(8,128)(2,1)S(1)}, u32[]{:S(2)}) copy-start(bf16[2,128,256]{2,1,0:T(8,128)(2,1)S(1)} %scatter.19.rel) | copy-start | bytes 393220
  64.1 45.0 %copy-start.4 = (bf16[192,768]{1,0:T(8,128)(2,1)}, bf16[192,768]{1,0:T(8,128)(2,1)S(1)}, u32[]{:S(2)}) copy-start(bf16[192,768]{1,0:T(8,128)(2,1)S(1)} %all_gather.23) | copy-start | bytes 884740
  112.4 55.8 %all-gather.11.cloned.1.call-start = ((), (), s32[]{:S(2)}) async-start(), calls=%async_computation.13 | async-start | bytes 1966080 | tf_op jit(solution)/shard_map/all_gather | solution.py:231
  114.0 32.8 %copy-start.19 = (f32[192]{0:T(256)}, f32[192]{0:T(256)S(1)}, u32[]{:S(2)}) copy-start(f32[192]{0:T(256)S(1)} %dynamic_slice.32) | copy-start | bytes 2308
  114.8 33.1 %copy-start.7 = (f32[768,384]{1,0:T(8,128)S(1)}, f32[768,384]{1,0:T(8,128)}, u32[]{:S(2)}) copy-start(f32[768,384]{1,0:T(8,128)} %param.46) | copy-start | bytes 3538948
  147.8 1.3 copy-start.1
  147.8 45.2 %all-gather.13.cloned.1.call-start = ((), (), s32[]{:S(2)}) async-start(), calls=%async_computation.14 | async-start | bytes 1769472 | tf_op jit(solution)/shard_map/all_gather | solution.py:244
  148.8 65.3 %all-gather.15.cloned.1.call-start = ((), (), s32[]{:S(2)}) async-start(), calls=%async_computation.15 | async-start | bytes 1966080 | tf_op jit(solution)/shard_map/all_gather | solution.py:231
  150.4 102.4 %reduce-scatter.29.cloned.1.call-start = ((), (), s32[]{:S(2)}) async-start(), calls=%async_computation.21 | async-start | bytes 1966080 | tf_op jit(solution)/shard_map/reduce_scatter | solution.py:234
  219.5 1.2 copy-start.33
  224.6 28.2 %copy-start.20 = (f32[192]{0:T(256)S(1)}, f32[192]{0:T(256)}, u32[]{:S(2)}) copy-start(f32[192]{0:T(256)} %copy-done.19) | copy-start | bytes 2308
  224.7 62.2 %all-gather.17.cloned.1.call-start = ((), (), s32[]{:S(2)}) async-start(), calls=%async_computation.16 | async-start | bytes 1966080 | tf_op jit(solution)/shard_map/all_gather | solution.py:231
  260.6 2.8 copy-start.15
  260.7 2.8 copy-start.17
  263.3 112.6 %reduce-scatter.35.cloned.1.call-start = ((), (), s32[]{:S(2)}) async-start(), calls=%async_computation.24 | async-start | bytes 1769472
  272.6 22.3 %all-to-all-start.2 = ((bf16[4,192,768]{2,1,0:T(8,128)(2,1)}), bf16[4,192,768]{2,1,0:T(8,128)(2,1)S(1)}, u32[]{:S(2)}, u32[]{:S(2)}) async-start(bf16[4,192,768]{2,1,0:T(8,128)(2,1)} %bitcast.90), calls=%async_computation.3 | async-start | bytes 2359296 | tf_op jit(solution)/shard_map/all_to_all | solution.py:303
  276.1 102.6 %reduce-scatter.33.cloned.1.call-start = ((), (), s32[]{:S(2)}) async-start(), calls=%async_computation.23 | async-start | bytes 589824
  291.7 88.8 %reduce-scatter.23.cloned.1.call-start = ((), (), s32[]{:S(2)}) async-start(), calls=%async_computation.18 | async-start | bytes 1769472 | tf_op jit(solution)/shard_map/reduce_scatter | solution.py:306
  295.9 86.0 %reduce-scatter.21.cloned.1.call-start = ((), (), s32[]{:S(2)}) async-start(), calls=%async_computation.17 | async-start | bytes 1474560 | tf_op jit(solution)/shard_map/reduce_scatter | solution.py:306
  296.2 44.1 %copy-start.31 = (bf16[768,1024]{1,0:T(8,128)(2,1)S(1)}, bf16[768,1024]{1,0:T(8,128)(2,1)}, u32[]{:S(2)}) copy-start(bf16[768,1024]{1,0:T(8,128)(2,1)} %all-gather.9.cloned.1.call-done) | copy-start | bytes 4718596
  362.0 50.4 %reduce-scatter.31.cloned.1.call-start = ((), (), s32[]{:S(2)}) async-start(), calls=%async_computation.22 | async-start | bytes 1966080 | tf_op jit(solution)/shard_map/reduce_scatter | solution.py:234
  366.3 1.3 copy-start.32
  366.3 98.3 %reduce-scatter.27.cloned.1.call-start = ((), (), s32[]{:S(2)}) async-start(), calls=%async_computation.20 | async-start | bytes 1966080 | tf_op jit(solution)/shard_map/reduce_scatter | solution.py:234
  374.3 1.1 copy-start.28
  374.3 1.3 copy-start.27
  374.3 3.8 copy-start.26
  374.3 4.0 copy-start.30
  374.3 4.2 copy-start.29
  374.4 149.7 %all-reduce.5.cloned.1.call-start = ((), (), s32[]{:S(2)}) async-start(), calls=%async_computation.25 | async-start | bytes 3637248 | tf_op jit(solution)/shard_map/psum | solution.py:306
  375.9 6.0 %copy-start.14 = (f32[2,128,256]{2,1,0:T(8,128)S(1)}, f32[2,128,256]{2,1,0:T(8,128)}, u32[]{:S(2)}) copy-start(f32[2,128,256]{2,1,0:T(8,128)} %get-tuple-element.70) | copy-start | bytes 786436
  381.9 30.6 %copy-start.25 = (f32[192]{0:T(256)S(1)}, f32[192]{0:T(256)}, u32[]{:S(2)}) copy-start(f32[192]{0:T(256)} %copy-done.24) | copy-start | bytes 2308
  381.9 82.7 %copy-start.3 = (bf16[192,1024]{1,0:T(8,128)(2,1)S(1)}, bf16[192,1024]{1,0:T(8,128)(2,1)}, u32[]{:S(2)}) copy-start(bf16[192,1024]{1,0:T(8,128)(2,1)} %reduce-scatter.29.cloned.1.call-done) | copy-start | bytes 1179652
  381.9 82.7 %copy-start.16 = (f32[1,1024]{1,0:T(1,128)S(1)}, f32[1,1024]{1,0:T(1,128)}, u32[]{:S(2)}) copy-start(f32[1,1024]{1,0:T(1,128)} %copy-done.15) | copy-start | bytes 12292
  381.9 82.7 %copy-start.18 = (f32[1,1024]{1,0:T(1,128)S(1)}, f32[1,1024]{1,0:T(1,128)}, u32[]{:S(2)}) copy-start(f32[1,1024]{1,0:T(1,128)} %copy-done.17) | copy-start | bytes 12292
  381.9 82.7 %copy-start.21 = (f32[192]{0:T(256)S(1)}, f32[192]{0:T(256)}, u32[]{:S(2)}) copy-start(f32[192]{0:T(256)} %copy-done.19) | copy-start | bytes 2308
  412.4 52.2 %copy-start.5 = (bf16[192,1024]{1,0:T(8,128)(2,1)S(1)}, bf16[192,1024]{1,0:T(8,128)(2,1)}, u32[]{:S(2)}) copy-start(bf16[192,1024]{1,0:T(8,128)(2,1)} %reduce-scatter.31.cloned.1.call-done) | copy-start | bytes 1179652
  526.5 2.1 copy-start.13
  (3 other events, 3.1 us)
Sparse Core Ops, SparseCore 0:
  12.1 36.5 all-gather.6
  50.8 28.1 all-gather.8
  112.6 27.0 reduce-scatter.24
  147.9 20.2 all-gather.10
  170.2 22.7 all-gather.12
  194.4 19.6 all-gather.14
  224.8 27.9 reduce-scatter.28
  263.5 23.2 all-gather.16
  289.1 21.8 reduce-scatter.34
  313.7 13.1 reduce-scatter.32
  329.7 21.8 reduce-scatter.22
  362.2 19.6 reduce-scatter.20
  384.4 27.9 reduce-scatter.30
  414.8 28.0 reduce-scatter.26
  446.5 77.5 all-reduce.4

commit v2 on v1

--- a/solution.py
+++ b/solution.py
@@ -237,6 +237,232 @@
     both=lax.psum(jnp.stack([jnp.sum(v,axis=0) for v in vals]),"row")
     return [both[i:i+1]/D for i in range(len(vals))]
 
+
+CH=4
+VM=pl.BlockSpec(memory_space=pltpu.VMEM)
+SEM=pltpu.SemaphoreType.DMA
+
+class Row:
+    def __init__(self):
+        self.me=lax.axis_index("row")
+        self.near=self.me+1-2*lax.rem(self.me,2)
+        self.far=lax.rem(self.me+2,4)
+        self.both=lax.rem(self.near+2,4)
+
+def send(src,dst,ssem,rsem,row,col=None):
+    where={"row":row} if col is None else {"row":row,"col":col}
+    return pltpu.make_async_remote_copy(src_ref=src,dst_ref=dst,send_sem=ssem,recv_sem=rsem,device_id=where,device_id_type=pl.DeviceIdType.MESH)
+
+def greet_row(p):
+    sem=pltpu.get_barrier_semaphore()
+    for peer in (p.near,p.far,p.both):
+        pl.semaphore_signal(sem,inc=1,device_id={"row":peer},device_id_type=pl.DeviceIdType.MESH)
+    pl.semaphore_wait(sem,3)
+
+class Gather:
+    def __init__(self,p,buf,sems,use):
+        self.p,self.buf,self.sems,self.use,self.flight=p,buf,sems,use,{}
+    def rows(self,t,b):
+        n=self.buf.shape[1]//4
+        return self.buf.at[t,pl.ds(pl.multiple_of(b*n,n),n)]
+    def start(self,t,value):
+        n=self.buf.shape[1]//4; p=self.p
+        self.buf[t,pl.ds(pl.multiple_of(p.me*n,n),n)]=value
+        mine=self.rows(t,p.me); s=lambda k:self.sems.at[self.use,t,k]
+        far=send(mine,mine,s(0),s(1),p.far); near=send(mine,mine,s(2),s(3),p.near)
+        far.start(); near.start()
+        self.flight[t]=[far,near]
+    def forward(self,t):
+        p=self.p; s=lambda k:self.sems.at[self.use,t,k]
+        self.flight[t][0].wait_recv()
+        got=self.rows(t,p.far)
+        on=send(got,got,s(4),s(5),p.near)
+        on.start(); self.flight[t].append(on)
+    def wait(self,t):
+        self.flight[t][1].wait_recv(); self.flight[t][2].wait_recv()
+        return self.buf[t]
+    def drain(self):
+        for copies in self.flight.values():
+            for c in copies: c.wait_send()
+
+class Scatter:
+    def __init__(self,p,part,s1,r1,s2,r2,sems,use):
+        self.p,self.part,self.s1,self.r1,self.s2,self.r2,self.sems,self.use,self.flight=p,part,s1,r1,s2,r2,sems,use,{}
+    def block(self,t,b):
+        n=self.part.shape[1]//4
+        return self.part[t,pl.ds(pl.multiple_of(b*n,n),n)]
+    def start(self,t):
+        p=self.p; u=self.use
+        self.s1[u,t,0]=self.block(t,p.near).astype(bf16)
+        self.s1[u,t,1]=self.block(t,p.both).astype(bf16)
+        c=send(self.s1.at[u,t],self.r1.at[u,t],self.sems.at[u,t,0],self.sems.at[u,t,1],p.near)
+        c.start(); self.flight[t]=[c]
+    def cross(self,t):
+        p=self.p; u=self.use
+        self.flight[t][0].wait_recv()
+        self.s2[u,t]=(self.block(t,p.far)+self.r1[u,t,1].astype(f32)).astype(bf16)
+        c=send(self.s2.at[u,t],self.r2.at[u,t],self.sems.at[u,t,2],self.sems.at[u,t,3],p.far)
+        c.start(); self.flight[t].append(c)
+    def wait(self,t):
+        u=self.use
+        self.flight[t][1].wait_recv()
+        return self.block(t,self.p.me)+self.r1[u,t,0].astype(f32)+self.r2[u,t].astype(f32)
+    def drain(self):
+        for copies in self.flight.values():
+            for c in copies: c.wait_send()
+
+class Totals:
+    def __init__(self,p,out,got,sems,use):
+        self.p,self.out,self.got,self.sems,self.use,self.flight=p,out,got,sems,use,{}
+    def start(self,t,a,b):
+        u=self.use; p=self.p
+        self.out[u,t,0:1]=jnp.sum(a,axis=0,keepdims=True)
+        self.out[u,t,1:2]=jnp.sum(b,axis=0,keepdims=True)
+        copies=[]
+        for i,peer in enumerate((p.near,p.far,p.both)):
+            c=send(self.out.at[u,t],self.got.at[u,t,i],self.sems.at[u,t,2*i],self.sems.at[u,t,2*i+1],peer)
+            c.start(); copies.append(c)
+        self.flight[t]=copies
+    def wait(self,t):
+        u=self.use
+        for c in self.flight[t]: c.wait_recv()
+        total=self.out[u,t]+self.got[u,t,0]+self.got[u,t,1]+self.got[u,t,2]
+        return total[0:1]/D,total[1:2]/D
+    def drain(self):
+        for copies in self.flight.values():
+            for c in copies: c.wait_send()
+
+def tiled(rows,step,body):
+    def run(i,carry):
+        body(pl.ds(pl.multiple_of(i*step,step),step))
+        return carry
+    lax.fori_loop(0,rows//step,run,0)
+
+def turn(dst,src):
+    m,n=src.shape
+    step=128 if m%128==0 else 64
+    for i in range(0,m,step):
+        dst[:,i:i+step]=src[i:i+step,:].T
+
+def mlp_kernel(x_ref,cot_ref,o_ref,wo,wu,wd,bo,g2,s2,bu,bd,
+               y_ref,dx1_ref,do_ref,dwo_ref,dwd_ref,dwu_ref,dg2_ref,ds2_ref,dbo_ref,dbd_ref,dbu_ref,
+               wot,wut,wdt,part,part2,a2,dyb,dat,gb,dhb,x1b,st,da2b,s1b,r1b,s2b,r2b,tout,tgot,gsem,ssem,tsem):
+    p=Row(); T=x_ref.shape[1]//CH
+    cols=lambda t:slice(T*t,T*(t+1))
+    greet_row(p)
+    out_sum=Scatter(p,part,s1b,r1b,s2b,r2b,ssem,0)
+    y_sum=Scatter(p,part2,s1b,r1b,s2b,r2b,ssem,1)
+    da_sum=Scatter(p,part,s1b,r1b,s2b,r2b,ssem,2)
+    ga,gy,gd=[Gather(p,b,gsem,i) for i,b in enumerate((a2,dyb,dat))]
+    st2,stb=Totals(p,tout,tgot,tsem,0),Totals(p,tout,tgot,tsem,1)
+    turn(wot,wo)
+    def project(t):
+        part[t]=nt(wot[...],o_ref[T*t:T*(t+1),:])
+        out_sum.start(t)
+    def residual(t):
+        x1=x_ref[:,cols(t)]+out_sum.wait(t)+bo[...]
+        x1b[t]=x1
+        st2.start(t,x1,x1*x1)
+    def second_norm(t):
+        m,sq=st2.wait(t)
+        inv=lax.rsqrt(sq-m*m+EPS)
+        st[t,0:1]=m; st[t,1:2]=inv
+        ga.start(t,((x1b[t]-m)*inv*g2[...]+s2[...]).astype(bf16))
+        gy.start(t,cot_ref[:,cols(t)].astype(bf16))
+    def hidden(t):
+        ga.wait(t); gy.wait(t)
+        def tile(r):
+            h=nn(wut[r,:],a2[t])+bu[r,:]
+            act,slope=gelu_parts(h)
+            gb[t,r]=act.astype(bf16)
+            dh=(nn(wd[r,:],dyb[t])*slope).astype(bf16)
+            dhb[t,r]=dh
+            dbu_ref[r,:]+=jnp.sum(dh.astype(f32),axis=1,keepdims=True)
+        tiled(wut.shape[0],128,tile)
+        def back(r):
+            part[t,r]=nn(wu[r,:],dhb[t])
+        tiled(wu.shape[0],256,back)
+        da_sum.start(t)
+    def down(t):
+        def tile(r):
+            part2[t,r]=nn(wdt[r,:],gb[t])
+        tiled(wdt.shape[0],256,tile)
+        y_sum.start(t)
+    def norm_of(t): return (x1b[t]-st[t,0:1])*st[t,1:2]
+    def second_back(t):
+        da2=da_sum.wait(t); norm=norm_of(t)
+        dg2_ref[...]+=jnp.sum(da2*norm,axis=1,keepdims=True)
+        ds2_ref[...]+=jnp.sum(da2,axis=1,keepdims=True)
+        e=da2*g2[...]
+        da2b[t]=e
+        stb.start(t,e,e*norm)
+    def middle(t):
+        u,w=stb.wait(t)
+        dx1=cot_ref[:,cols(t)]+st[t,1:2]*(da2b[t]-u-norm_of(t)*w)
+        dx1_ref[:,cols(t)]=dx1
+        low=dx1.astype(bf16)
+        dbo_ref[...]+=jnp.sum(low.astype(f32),axis=1,keepdims=True)
+        gd.start(t,low)
+    def attended(t):
+        gd.wait(t)
+        do_ref[:,cols(t)]=nn(wo[...],dat[t]).astype(bf16)
+    def finish(t):
+        y_ref[:,cols(t)]=x1b[t]+y_sum.wait(t)+bd[...]
+    for ref in (dg2_ref,ds2_ref,dbo_ref,dbd_ref,dbu_ref): ref[...]=jnp.zeros(ref.shape,f32)
+    def weight_grads():
+        def one(r):
+            acc=None; acc2=None
+            for t in range(CH):
+                v=nt(gb[t,r],dyb[t]); acc=v if acc is None else acc+v
+                v=nt(a2[t,r],dhb[t]); acc2=v if acc2 is None else acc2+v
+            dwd_ref[r,:]=acc.astype(bf16)
+            dwu_ref[r,:]=acc2.astype(bf16)
+        tiled(dwd_ref.shape[0],128,one)
+    for t in range(CH): project(t)
+    for t in range(CH): out_sum.cross(t)
+    turn(wut,wu); turn(wdt,wd)
+    for t in range(CH):
+        residual(t)
+        if t>0: second_norm(t-1)
+    second_norm(CH-1)
+    for t in range(CH):
+        ga.forward(t); gy.forward(t)
+        hidden(t)
+        if t>0: da_sum.cross(t-1)
+    down(0); da_sum.cross(CH-1)
+    for t in range(1,CH): down(t)
+    for t in range(CH):
+        second_back(t)
+        if t>0: middle(t-1)
+    middle(CH-1)
+    for t in range(CH): y_sum.cross(t)
+    for t in range(CH): dbd_ref[...]+=jnp.sum(cot_ref[:,cols(t)].astype(bf16).astype(f32),axis=1,keepdims=True)
+    for t in range(CH): gd.forward(t)
+    weight_grads()
+    for t in range(CH): attended(t)
+    acc=None
+    for t in range(CH):
+        v=nt(o_ref[T*t:T*(t+1),:].T,dat[t]); acc=v if acc is None else acc+v
+    dwo_ref[...]=acc.astype(bf16)
+    for t in range(CH): finish(t)
+    for c in (out_sum,y_sum,da_sum,ga,gy,gd,st2,stb): c.drain()
+
+def mlp_block(x,cot,o,wo,wu,wd,bo,g2,s2,bu,bd):
+    w,n=x.shape; T=n//CH; hid=wu.shape[1]; d=wu.shape[0]
+    sd=jax.ShapeDtypeStruct; V=pltpu.VMEM
+    return pl.pallas_call(mlp_kernel,name="mlp_block",
+      out_shape=(sd((w,n),f32),sd((w,n),f32),sd((w,n),bf16),sd(wo.shape,bf16),sd((hid,d),bf16),sd((d,hid),bf16),
+                 sd((w,1),f32),sd((w,1),f32),sd((w,1),f32),sd((w,1),f32),sd((hid,1),f32)),
+      in_specs=[VM]*11,out_specs=(VM,)*11,
+      scratch_shapes=[V((d,w),bf16),V((hid,d),bf16),V((d,hid),bf16),V((CH,d,T),f32),V((CH,d,T),f32),
+        V((CH,d,T),bf16),V((CH,d,T),bf16),V((CH,d,T),bf16),V((CH,hid,T),bf16),V((CH,hid,T),bf16),
+        V((CH,w,T),f32),V((CH,8,T),f32),V((CH,w,T),f32),
+        V((3,CH,2,w,T),bf16),V((3,CH,2,w,T),bf16),V((3,CH,w,T),bf16),V((3,CH,w,T),bf16),
+        V((2,CH,8,T),f32),V((2,CH,3,8,T),f32),SEM((3,CH,6)),SEM((3,CH,4)),SEM((2,CH,6))],
+      cost_estimate=pl.CostEstimate(flops=8*10**9,bytes_accessed=3*10**7,transcendentals=10**6),
+      compiler_params=pltpu.CompilerParams(collective_id=1,has_side_effects=True,vmem_limit_bytes=60<<20),
+    )(x,cot,o,wo,wu,wd,bo,g2,s2,bu,bd)
+
 def local(tokens,cotangent,offsets,ln1_gain,ln1_bias,q_weight,k_weight,v_weight,q_bias,v_bias,rel_pos_h,rel_pos_w,
           out_weight,out_bias,ln2_gain,ln2_bias,up_weight,up_bias,down_weight,down_bias):
     rows=lax.axis_size("row"); r=lax.axis_index("row"); cols=lax.axis_size("col")
@@ -265,31 +491,9 @@
     a1=gather_rows((norm1*g1+s1).astype(bf16))
     qkv=(tn(w_qkv,a1)+b_qkv).astype(bf16)
     o=attend(offsets,qkv,rel)
-    x1=x+sum_rows(lax.dot_general(w_out,o,(((0,),(1,)),((),())),preferred_element_type=f32))+b_out
-    m2,sq2=row_stats(x1,x1*x1)
-    inv2=lax.rsqrt(sq2-m2*m2+EPS); norm2=(x1-m2)*inv2
-    a2=gather_rows((norm2*g2+s2).astype(bf16))
-    h=tn(w_up,a2)+b_up
-    act,slope=gelu_parts(h)
-    g=act.astype(bf16)
-    output=x1+sum_rows(tn(w_down,g))+b_down
-    dy_own=cotangent.astype(bf16)
-    dy=gather_rows(dy_own)
-    d_down_bias=jnp.sum(dy_own,axis=1,dtype=f32)
-    dh=(nn(w_down,dy)*slope).astype(bf16)
-    d_down=nt(g,dy).astype(bf16)
-    d_up=nt(a2,dh).astype(bf16)
-    d_up_bias=jnp.sum(dh,axis=1,dtype=f32)
-    da2=sum_rows(nn(w_up,dh))
-    d_g2=jnp.sum(da2*norm2,axis=1); d_s2=jnp.sum(da2,axis=1)
-    e2=da2*g2
-    u,w=row_stats(e2,e2*norm2)
-    dx1=cotangent+inv2*(e2-u-norm2*w)
-    dat_own=dx1.astype(bf16)
-    d_out_bias=jnp.sum(dat_own,axis=1,dtype=f32)
-    dat=gather_rows(dat_own)
-    d_out=lax.dot_general(o,dat,(((0,),(1,)),((),())),preferred_element_type=f32).astype(bf16)
-    do=nn(w_out,dat).astype(bf16)
+    output,dx1,do,d_out,d_down,d_up,d_g2,d_s2,d_out_bias,d_down_bias,d_up_bias=mlp_block(
+        x,cotangent,o,w_out,w_up,w_down,b_out,g2,s2,b_up,b_down)
+    d_g2,d_s2,d_out_bias,d_down_bias,d_up_bias=[v[:,0] for v in (d_g2,d_s2,d_out_bias,d_down_bias,d_up_bias)]
     dqkv,drel=attend_back(offsets,qkv,do,rel)
     d_qkv=nn(a1,dqkv).astype(bf16)
     b_sums=head_unorder(jnp.sum(dqkv,axis=0,dtype=f32))

time: 548 us -> 429 us (0.78); the launches traced: 540 us -> 428 us
  waiting for transfers between devices: 258 us -> 108 us
  Pallas kernels: 58.5 us -> 137 us
  matrix products: 46 us -> 9.63 us
  blocking collectives: 92.7 us -> 104 us
  other arithmetic: 27.7 us -> 17.5 us
    pallas_call x0 -> x1, Pallas kernels: none -> 78.6 us  [mlp_block(): pl.pallas_call(mlp_kernel, name='mlp_block', out_shape=(sd((w, n), f32),...]
    all_gather x4 -> x1, waiting for transfers between devices: 61.8 us -> 0.01 us  [gather_rows(): return lax.all_gather(block, 'row', axis=0, tiled=True)]
    reduce_scatter x4 -> x1, waiting for transfers between devices: 81.4 us -> 27.4 us  [sum_rows(): lax.psum_scatter(partial.astype(bf16), 'row', scatter_dimension=0, tiled=...]
    psum x1, waiting for transfers between devices: 56.8 us -> 26.1 us  [reduce(): lax.psum(lax.psum_scatter(t, 'col', scatter_dimension=axis, tiled=True),...]
    all_to_all x1 -> x2, blocking collectives: 16.9 us -> 37.2 us  [turn_back(): lax.all_to_all(dw.reshape(rows, width, n), 'row', split_axis=0, concat_ax...]
    all_gather x1, waiting for transfers between devices: 18.8 us -> 0.01 us  [local(): lax.all_gather(w.astype(bf16), 'col', axis=1, tiled=True)]
    reduce_scatter x2, waiting for transfers between devices: 1.42 us -> 16 us  [reduce(): lax.psum_scatter(t, 'col', scatter_dimension=axis, tiled=True)]
    psum x4 -> x2, blocking collectives: 27.4 us -> 14.8 us  [row_stats(): both = lax.psum(jnp.stack([jnp.sum(v, axis=0) for v in vals]), 'row')]
  transfers between devices with their start and end apart: 17 -> 10, of which waited for: 13 -> 5; matrix products, arithmetic and copies ran while one was open for 12% -> 10% of each run, Pallas kernels for 8% -> 14%
where the time goes in v2:
time: 429 us; the launch traced here: 428 us
  Pallas kernels  137 us (32%)
  waiting for transfers between devices  108 us (25%)
  blocking collectives  104 us (24%)
  local copies, waits for them, and re-layouts  32.6 us (8%)
  other arithmetic  17.5 us (4%)
  between operations  14.4 us (3%)
  matrix products  9.63 us (2%)
    pallas_call x1, Pallas kernels, mlp_block(): pl.pallas_call(mlp_kernel, name='mlp_block', out_shape=(sd((w, n), f32),...  78.6 us
    psum x1, blocking collectives, local(): lax.psum((spread(d_g1, D, r), spread(d_s1, D, r), spread(b_sums[0], D, r)...  44.9 us
    pallas_call x1, Pallas kernels, attend_back(): pl.pallas_call(bwd_kernel, out_shape=(jax.ShapeDtypeStruct((1024, 576), b...  41.3 us
    all_to_all x2, blocking collectives, turn_back(): lax.all_to_all(dw.reshape(rows, width, n), 'row', split_axis=0, concat_ax...  37.2 us
    reduce_scatter x1, waiting for transfers between devices, sum_rows(): lax.psum_scatter(partial.astype(bf16), 'row', scatter_dimension=0, tiled=...  27.4 us
    psum x1, waiting for transfers between devices, reduce(): lax.psum(lax.psum_scatter(t, 'col', scatter_dimension=axis, tiled=True),...  26.1 us
    all_gather x1, waiting for transfers between devices, local(): full = lax.all_gather(own, 'col', axis=1, tiled=True)  25.5 us
    pallas_call x1, Pallas kernels, attend(): pl.pallas_call(fwd_kernel, out_shape=jax.ShapeDtypeStruct((1024, 192), bf...  17.5 us
  transfers between devices with their start and end apart: 10, of which 5 were waited for; matrix products, arithmetic and copies ran while one was open for 10% of the time, Pallas kernels for 14%

profile of v2, /device:TPU:0, one launch (start us, length us, event | category | flops | bytes accessed | tf_op | source)
XLA Modules:
  0.0 427.9 jit_solution(15662641964634825586)
XLA Ops:
  7.3 1.1 convert.17
  8.3 1.0 convert.18
  10.8 1.1 pad_maximum_fusion.1
  13.7 8.5 %psum.119 = f32[2,1024]{1,0:T(2,128)S(1)} all-reduce(f32[2,1024]{1,0:T(2,128)S(1)} %pad_maximum_fusion.5), channel_id=1, replica_groups=mesh['dp'=4,'row'=4,'col'=2] {'row'}, use_global_device_ids=true, to_apply=%region_2.0 | all-reduce | flops 2048 | bytes 16384 | tf_op jit(solution)/shard_map/psum | solution.py:237
  22.2 1.0 add_convert_fusion.1
  23.2 25.5 %all-gather.4.cloned.1.call-done = bf16[192,4,1344]{2,0,1:T(8,128)(2,1)} async-done(((bf16[192,2,1344]{2,0,1:T(8,128)(2,1)}), bf16[192,4,1344]{2,0,1:T(8,128)(2,1)}) %all-gather.4.cloned.1.call-update) | async-done | bytes 2064400 | tf_op jit(solution)/shard_map/all_gather | solution.py:478
  48.7 3.6 all-to-all-start
  52.4 0.9 convert_element_type.55
  53.3 0.8 dynamic_slice.29
  55.3 0.8 dynamic_slice.31
  56.1 0.8 copy.56.bo
  57.6 0.8 copy.57.g2
  60.7 0.8 copy.60.bd
  61.4 0.8 dynamic_slice.34
  62.2 1.0 broadcast_in_dim.38.bu
  65.4 6.9 %all_gather.14.wo = bf16[192,768]{1,0:T(8,128)(2,1)} all-gather(bf16[192,384]{1,0:T(8,128)(2,1)S(1)} %convert_element_type.54), channel_id=1, replica_groups=mesh['dp'=4,'row'=4,'col'=2] {'col'}, dimensions={1}, use_global_device_ids=true | all-gather | bytes 442368 | tf_op jit(solution)/shard_map/all_gather | solution.py:470
  72.9 1.0 fusion.19.cells
  73.8 13.3 %all-to-all-done = bf16[192,4,1344]{2,0,1:T(8,128)(2,1)S(1)} async-done(((bf16[192,4,1344]{2,0,1:T(8,128)(2,1)}), bf16[192,4,1344]{2,0,1:T(8,128)(2,1)S(1)}, u32[]{:S(2)}, u32[]{:S(2)}) %all-to-all-start) | async-done | bytes 2064416 | tf_op jit(solution)/shard_map/all_to_all | solution.py:479
  87.1 1.5 slice.358.wu
  88.6 3.7 add_convert_fusion.qkv
  92.3 17.5 %attend.1.o_ref = bf16[1024,192]{1,0:T(8,128)(2,1)} custom-call(s32[1,2]{1,0:T(1,128)} %off.3, bf16[576,1024]{1,0:T(8,128)(2,1)} %add_convert_fusion.qkv, bf16[2,128,256]{2,1,0:T(8,128)(2,1)} %copy-done.6, s32[384,1]{1,0:T(8,128)} %fusion.19.cells, s32[1,256]{1,0:T(1,128)} %fusion.28.toks), custom_call_target="tpu_custom_call" | custom-call | tf_op jit(solution)/shard_map/attend/pallas_call | solution.py:128
  109.8 78.6 %mlp_block.1 = (f32[192,1024]{1,0:T(8,128)}, f32[192,1024]{1,0:T(8,128)}, bf16[192,1024]{1,0:T(8,128)(2,1)}, bf16[192,768]{1,0:T(8,128)(2,1)}, bf16[768,768]{1,0...) custom-call(f32[192,1024]{1,0:T(8,128)} %x_ref.1, ...), custom_call_target="tpu_custom_call" | custom-call | flops 8000000000 | bytes 30000000 | tf_op jit(solution)/shard_map/mlp_block/pallas_call | solution.py:453
  188.4 1.9 copy.64
  190.4 2.4 copy.66
  193.0 41.3 %attend_back.1 = (bf16[1024,576]{1,0:T(8,128)(2,1)}, f32[2,128,256]{2,1,0:T(8,128)}) custom-call(s32[1,2]{1,0:T(1,128)} %off.3, bf16[576,1024]{1,0:T(8,128)(2,1)} %add_convert_fusion.qkv, bf16[192,1024]{1,0:T(8,128)(2,1)} %get-tuple-element.82.do, bf16[2,128,256]{2,1,0:T(8,128)(2,1)} %copy-done.6, s32[384,1]{1,0:T(8,128)} %fusion.19.cells, s32[1,256]{1,0:T(1,128)} %fusion.28.toks), custom_call_target="tpu_custom_call" | custom-call | tf_op jit(solution)/shard_map/attend_back/pallas_call | solution.py:196
  234.3 3.4 convolution_convert_fusion.1
  237.7 1.5 copy.61
  239.2 16.9 %all_to_all.25 = bf16[4,192,576]{2,1,0:T(8,128)(2,1)} all-to-all(bf16[4,192,576]{2,1,0:T(8,128)(2,1)S(1)} %bitcast.59), channel_id=1, replica_groups=mesh['dp'=4,'row'=4,'col'=2] {'row'}, dimensions={0} | all-to-all | bytes 1769472 | tf_op jit(solution)/shard_map/all_to_all | solution.py:507
  256.2 20.3 %all_to_all.26 = bf16[4,192,768]{2,1,0:T(8,128)(2,1)} all-to-all(bf16[4,192,768]{2,1,0:T(8,128)(2,1)} %bitcast.63), channel_id=1, replica_groups=mesh['dp'=4,'row'=4,'col'=2] {'row'}, dimensions={0} | all-to-all | bytes 2359296 | tf_op jit(solution)/shard_map/all_to_all | solution.py:507
  276.6 2.6 convolution_convert_fusion
  279.3 1.7 copy.65
  281.0 2.2 copy.67
  283.2 16.0 %reduce-scatter.14.cloned.1.call-done = bf16[2,192,768]{2,1,0:T(8,128)(2,1)} async-done(((bf16[4,192,768]{2,1,0:T(8,128)(2,1)}), bf16[2,192,768]{2,1,0:T(8,128)(2,1)}) %reduce-scatter.14.cloned.1.call-update) | async-done | bytes 589840 | tf_op jit(solution)/shard_map/reduce_scatter | solution.py:510
  302.3 27.4 %reduce-scatter.10.cloned.1.call-done = bf16[192,1024]{1,0:T(8,128)(2,1)} async-done(((bf16[768,1024]{1,0:T(8,128)(2,1)}), bf16[192,1024]{1,0:T(8,128)(2,1)}) %reduce-scatter.10.cloned.1.call-update) | async-done | bytes 393232 | tf_op jit(solution)/shard_map/reduce_scatter | solution.py:234
  329.7 1.4 fusion.9
  331.6 44.9 %all-reduce.1 = (f32[768]{0:T(1024)}, f32[768]{0:T(1024)}, f32[768]{0:T(1024)}, f32[768]{0:T(1024)}, f32[27,64]{0,1:T(8,128)S(1)}, /*index=5*/f32[27,64]{0,1:T(8...) all-reduce(f32[768]{0:T(1024)S(1)} %dynamic_update_slice.27, ...), channel_id=1, replica_groups=mesh['dp'=4,'row'=4,'col'=2] {'dp','row','col'}, use_global_device_ids=true, to_apply=%region_8.9 | all-reduce | flops 12672 | bytes 101376 | tf_op jit(solution)/shard_map/psum | solution.py:517
  377.9 6.3 %psum.120 = f32[2,1024]{1,0:T(2,128)S(1)} all-reduce(f32[2,1024]{1,0:T(2,128)S(1)} %pad_maximum_fusion.6), channel_id=1, replica_groups=mesh['dp'=4,'row'=4,'col'=2] {'row'}, use_global_device_ids=true, to_apply=%region_6.0 | all-reduce | flops 2048 | bytes 16384 | tf_op jit(solution)/shard_map/psum | solution.py:237
  384.3 1.1 fusion.8
  385.4 26.1 %all-reduce.5.cloned.1.call-done = (bf16[2,192,576]{2,1,0:T(8,128)(2,1)}, bf16[192,384]{1,0:T(8,128)(2,1)}, bf16[2,192,768]{2,1,0:T(8,128)(2,1)}, bf16[768,384]{1,0:T(8,128)(2,1)}) async-done(((bf16[2,192,576]{2,1,0:T(8,128)(2,1)}, bf16[192,384]{1,0:T(8,128)(2,1)}, bf16[2,192,768]{2,1,0:T(8,128)(2,1)}, bf16[768,384]{1,0:T(8,128)(2,1)}), (bf16[2,192,576]{2,1,0:T(8,128)(2,1)}, bf16[192,384]{1,0:T(8,128)(2,1)}, ...) | async-done | bytes 1769488 | tf_op jit(solution)/shard_map/psum | solution.py:510
  411.5 1.1 convert_element_type.59
  413.0 0.8 copy-done.10
  414.0 1.0 copy-done.9
  414.9 1.1 convert_element_type.63
  416.7 1.2 pad_maximum_fusion
  417.9 0.9 pad_maximum_fusion.4
  418.8 0.9 pad_maximum_fusion.3
  419.6 0.9 pad_maximum_fusion.2
  420.5 0.9 copy.85
  (144 shorter events, 16.9 us)
Async XLA Ops:
  7.2 2.3 copy-start.12
  7.2 2.5 copy-start.4
  7.2 41.5 %all-gather.4.cloned.1.call-start = ((), (), s32[]{:S(2)}) async-start(), calls=%async_computation.8 | async-start | bytes 3244032 | tf_op jit(solution)/shard_map/all_gather | solution.py:478
  10.8 2.7 copy-start
  12.0 76.6 %all-gather.6.cloned.1.call-start = ((), (), s32[]{:S(2)}) async-start(), calls=%async_computation.9 | async-start | bytes 1966080 | tf_op jit(solution)/shard_map/all_gather | solution.py:231
  23.2 29.2 %copy-start.5 = (f32[768,384]{1,0:T(8,128)S(1)}, f32[768,384]{1,0:T(8,128)}, u32[]{:S(2)}) copy-start(f32[768,384]{1,0:T(8,128)} %param.46) | copy-start | bytes 3538948
  48.7 38.4 %all-to-all-start = ((bf16[192,4,1344]{2,0,1:T(8,128)(2,1)}), bf16[192,4,1344]{2,0,1:T(8,128)(2,1)S(1)}, u32[]{:S(2)}, u32[]{:S(2)}) async-start(bf16[192,4,1344]{2,0,1:T(8,128)(2,1)} %all-gather.4.cloned.1.call-done), calls=%async_computation | async-start | bytes 4325376 | tf_op jit(solution)/shard_map/all_to_all | solution.py:479
  52.3 2.6 copy-start.20
  52.3 2.8 copy-start.21
  52.3 57.4 %all-gather.8.cloned.1.call-start = ((), (), s32[]{:S(2)}) async-start(), calls=%async_computation.10 | async-start | bytes 1769472 | tf_op jit(solution)/shard_map/all_gather | solution.py:470
  53.3 9.9 %copy-start.13 = (f32[192,384]{1,0:T(8,128)S(1)}, f32[192,384]{1,0:T(8,128)}, u32[]{:S(2)}) copy-start(f32[192,384]{1,0:T(8,128)} %param.40) | copy-start | bytes 884740
  53.3 226.0 %reduce-scatter.16.cloned.1.call-start = ((), (), s32[]{:S(2)}) async-start(), calls=%async_computation.14 | async-start | bytes 589824
  65.3 23.3 %copy-start.6 = (bf16[2,128,256]{2,1,0:T(8,128)(2,1)}, bf16[2,128,256]{2,1,0:T(8,128)(2,1)S(1)}, u32[]{:S(2)}) copy-start(bf16[2,128,256]{2,1,0:T(8,128)(2,1)S(1)} %scatter.19.rel) | copy-start | bytes 393220
  190.3 90.7 %reduce-scatter.18.cloned.1.call-start = ((), (), s32[]{:S(2)}) async-start(), calls=%async_computation.15 | async-start | bytes 1769472
  192.8 90.4 %reduce-scatter.12.cloned.1.call-start = ((), (), s32[]{:S(2)}) async-start(), calls=%async_computation.12 | async-start | bytes 1474560 | tf_op jit(solution)/shard_map/reduce_scatter | solution.py:510
  193.0 41.3 %copy-start.22 = (bf16[768,1024]{1,0:T(8,128)(2,1)S(1)}, bf16[768,1024]{1,0:T(8,128)(2,1)}, u32[]{:S(2)}) copy-start(bf16[768,1024]{1,0:T(8,128)(2,1)} %all-gather.6.cloned.1.call-done) | copy-start | bytes 4718596
  256.1 43.0 %reduce-scatter.14.cloned.1.call-start = ((), (), s32[]{:S(2)}) async-start(), calls=%async_computation.13 | async-start | bytes 1769472 | tf_op jit(solution)/shard_map/reduce_scatter | solution.py:510
  256.2 20.4 %copy-start.3 = (bf16[1024,576]{1,0:T(8,128)(2,1)S(1)}, bf16[1024,576]{1,0:T(8,128)(2,1)}, u32[]{:S(2)}) copy-start(bf16[1024,576]{1,0:T(8,128)(2,1)} %get-tuple-element.83) | copy-start | bytes 3538948
  276.5 53.2 %reduce-scatter.10.cloned.1.call-start = ((), (), s32[]{:S(2)}) async-start(), calls=%async_computation.11 | async-start | bytes 1966080 | tf_op jit(solution)/shard_map/reduce_scatter | solution.py:234
  279.2 132.3 %all-reduce.5.cloned.1.call-start = ((), (), s32[]{:S(2)}) async-start(), calls=%async_computation.16 | async-start | bytes 3637248 | tf_op jit(solution)/shard_map/psum | solution.py:510
  281.0 18.2 %copy-start.19 = (f32[2,128,256]{2,1,0:T(8,128)S(1)}, f32[2,128,256]{2,1,0:T(8,128)}, u32[]{:S(2)}) copy-start(f32[2,128,256]{2,1,0:T(8,128)} %get-tuple-element.84) | copy-start | bytes 786436
  283.2 16.3 %copy-start.11 = (f32[768,1]{1,0:T(8,128)S(1)}, f32[768,1]{1,0:T(8,128)}, u32[]{:S(2)}) copy-start(f32[768,1]{1,0:T(8,128)} %get-tuple-element.90) | copy-start | bytes 9220
  283.2 16.5 %copy-start.18 = (f32[192,1]{1,0:T(8,128)S(1)}, f32[192,1]{1,0:T(8,128)}, u32[]{:S(2)}) copy-start(f32[192,1]{1,0:T(8,128)} %get-tuple-element.86) | copy-start | bytes 2308
  299.2 0.9 copy-start.17
  299.2 1.0 copy-start.16
  299.2 1.1 copy-start.15
  299.2 30.5 %copy-start.1 = (f32[192,1024]{1,0:T(8,128)S(1)}, f32[192,1024]{1,0:T(8,128)}, u32[]{:S(2)}) copy-start(f32[192,1024]{1,0:T(8,128)} %x_ref.1) | copy-start | bytes 2359300
  301.6 82.6 %copy-start.8 = (f32[192,1024]{1,0:T(8,128)S(1)}, f32[192,1024]{1,0:T(8,128)}, u32[]{:S(2)}) copy-start(f32[192,1024]{1,0:T(8,128)} %get-tuple-element.81) | copy-start | bytes 2359300
  329.7 54.5 %copy-start.2 = (bf16[192,1024]{1,0:T(8,128)(2,1)S(1)}, bf16[192,1024]{1,0:T(8,128)(2,1)}, u32[]{:S(2)}) copy-start(bf16[192,1024]{1,0:T(8,128)(2,1)} %reduce-scatter.10.cloned.1.call-done) | copy-start | bytes 1179652
  412.7 1.1 copy-start.10
  413.9 1.1 copy-start.9
  414.0 2.1 copy-start.14
  417.9 2.6 copy-start.7
Sparse Core Ops, SparseCore 0:
  12.1 36.5 all-gather.3
  50.8 28.1 all-gather.5
  81.1 22.7 all-gather.7
  190.4 12.3 reduce-scatter.15
  205.5 21.8 reduce-scatter.17
  256.2 18.7 reduce-scatter.11
  277.3 21.8 reduce-scatter.13
  301.7 27.9 reduce-scatter.9
  332.9 78.5 all-reduce.4

commit v3 on v2

--- a/solution.py
+++ b/solution.py
@@ -332,6 +332,156 @@
         for copies in self.flight.values():
             for c in copies: c.wait_send()
 
+class Turn:
+    def __init__(self,p,src,dst,sems):
+        n=src.shape[0]//4
+        rows=lambda b:src.at[pl.ds(pl.multiple_of(b*n,n),n)]
+        self.copies=[]
+        for i,peer in enumerate((p.far,p.both,p.near)):
+            c=send(rows(peer),dst.at[p.me],sems.at[2*i],sems.at[2*i+1],peer)
+            c.start(); self.copies.append(c)
+        self.own=pltpu.make_async_copy(rows(p.me),dst.at[p.me],sems.at[6])
+        self.own.start()
+    def wait(self):
+        for c in self.copies: c.wait_recv()
+        for c in self.copies: c.wait_send()
+        self.own.wait()
+
+def greet(others):
+    sem=pltpu.get_barrier_semaphore()
+    for where in others:
+        pl.semaphore_signal(sem,inc=1,device_id=where,device_id_type=pl.DeviceIdType.MESH)
+    pl.semaphore_wait(sem,len(others))
+
+def head_kernel(ncol,x_ref,oq_ref,ou_ref,g1,s1,bq,a1,qkv_ref,wq,wu,st,wqt,tout,tgot,gsem,tsem,ssem,rsem):
+    p=Row(); T=x_ref.shape[1]//CH; per=4//ncol
+    c=lax.axis_index("col")
+    cols=lambda t:slice(T*t,T*(t+1))
+    greet([{"row":lax.rem(p.me+i,4),"col":lax.rem(c+j,ncol)} for i in range(4) for j in range(ncol) if i or j])
+    def push(k,own,full):
+        for j in range(per):
+            row=per*c+j
+            for dc in range(ncol):
+                copy=send(own.at[j],full.at[p.me],ssem.at[k,j,dc],rsem.at[k,p.me],row,lax.rem(c+dc,ncol))
+                if dc: copy.start()
+                else:
+                    pl.when(row!=p.me)(copy.start)
+                    pl.when(row==p.me)(pltpu.make_async_copy(own.at[j],full.at[p.me],rsem.at[k,p.me]).start)
+    def arrive(k,own,full):
+        for s in range(4):
+            mine=jnp.logical_and(p.me==s,c==s//per)
+            local_copy=pltpu.make_async_copy(own.at[0],full.at[s],rsem.at[k,s])
+            remote=send(own.at[0],full.at[s],ssem.at[k,0,0],rsem.at[k,s],lax.rem(p.me+1,4),c)
+            pl.when(mine)(local_copy.wait)
+            pl.when(jnp.logical_not(mine))(remote.wait_recv)
+    def sent(k,own,full):
+        for j in range(per):
+            row=per*c+j
+            for dc in range(ncol):
+                copy=send(own.at[j],full.at[p.me],ssem.at[k,j,dc],rsem.at[k,p.me],row,lax.rem(c+dc,ncol))
+                if dc: copy.wait_send()
+                else: pl.when(row!=p.me)(copy.wait_send)
+    push(0,oq_ref,wq)
+    tot=Totals(p,tout,tgot,tsem,0); ga=Gather(p,a1,gsem,0)
+    for t in range(CH):
+        v=x_ref[:,cols(t)]
+        tot.start(t,v,v*v)
+    for t in range(CH):
+        m,sq=tot.wait(t)
+        inv=lax.rsqrt(sq-m*m+EPS)
+        st[t,0:1]=m; st[t,1:2]=inv
+        ga.start(t,((x_ref[:,cols(t)]-m)*inv*g1[...]+s1[...]).astype(bf16))
+    push(1,ou_ref,wu)
+    arrive(0,oq_ref,wq)
+    n=wq.shape[1]
+    for s in range(4): wqt[:,n*s:n*s+n]=wq[s].T
+    for t in range(CH): ga.forward(t)
+    for t in range(CH):
+        ga.wait(t)
+        def tile(r):
+            qkv_ref[r,cols(t)]=(nn(wqt[r,:],a1[t])+bq[r,:]).astype(bf16)
+        tiled(wqt.shape[0],192,tile)
+    arrive(1,ou_ref,wu)
+    sent(0,oq_ref,wq); sent(1,ou_ref,wu)
+    for q in (tot,ga): q.drain()
+
+def head_block(x,oq,ou,g1,s1,bq,ncol):
+    w,n=x.shape; T=n//CH; d=4*w; sd=jax.ShapeDtypeStruct; V=pltpu.VMEM
+    nq=oq.shape[2]; per=4//ncol
+    return pl.pallas_call(functools.partial(head_kernel,ncol),name="head_block",
+      out_shape=(sd((CH,d,T),bf16),sd((nq,n),bf16),sd((4,w,nq),bf16),sd((4,w,ou.shape[2]),bf16),sd((CH,8,T),f32)),
+      in_specs=[VM]*6,out_specs=(VM,)*5,
+      scratch_shapes=[V((nq,d),bf16),V((1,CH,8,T),f32),V((1,CH,3,8,T),f32),SEM((1,CH,6)),SEM((1,CH,6)),SEM((2,per,ncol)),SEM((2,4))],
+      cost_estimate=pl.CostEstimate(flops=10**9,bytes_accessed=10**8,transcendentals=0),
+      compiler_params=pltpu.CompilerParams(collective_id=2,has_side_effects=True,vmem_limit_bytes=48<<20),
+    )(x,oq,ou,g1,s1,bq)
+
+def tail_kernel(ncol,dqkv,wq,a1,x_ref,st,dx1,g1,dwo,in_ref,q_out,o_out,dg1,ds1,
+                part,s1b,r1b,s2b,r2b,tout,tgot,eb,dwq,tq,yq,yo,ssem,tsem,usem,ysem):
+    p=Row(); T=x_ref.shape[1]//CH; per=4//ncol
+    c=lax.axis_index("col"); other=ncol-1-c
+    cols=lambda t:slice(T*t,T*(t+1))
+    greet([{"row":q,"col":c} for q in (p.near,p.far,p.both)]+[{"row":p.me,"col":other}])
+    half=dwo.shape[1]//ncol
+    lanes=lambda k:pl.ds(pl.multiple_of(k*half,128),half)
+    out_copy=send(dwo.at[:,lanes(other)],yo,ysem.at[0],ysem.at[1],p.me,other)
+    out_copy.start()
+    def grads(r):
+        acc=None
+        for t in range(CH):
+            v=nn(a1[t,r],dqkv[T*t:T*(t+1),:]); acc=v if acc is None else acc+v
+        dwq[r,:]=acc.astype(bf16)
+    tiled(dwq.shape[0],192,grads)
+    turned=Turn(p,dwq,tq,usem)
+    total=Scatter(p,part,s1b,r1b,s2b,r2b,ssem,0); stats=Totals(p,tout,tgot,tsem,0)
+    for t in range(CH):
+        def tile(r):
+            part[t,r]=nt(wq[r,:],dqkv[T*t:T*(t+1),:])
+        tiled(wq.shape[0],192,tile)
+        total.start(t)
+        if t: total.cross(t-1)
+    total.cross(CH-1)
+    turned.wait()
+    block=lambda k:tq.at[pl.ds(per*k,per)]
+    q_copy=send(block(other),yq,ysem.at[2],ysem.at[3],p.me,other)
+    q_copy.start()
+    dg1[...]=jnp.zeros(dg1.shape,f32); ds1[...]=jnp.zeros(ds1.shape,f32)
+    norm_of=lambda t:(x_ref[:,cols(t)]-st[t,0:1])*st[t,1:2]
+    def first(t):
+        da=total.wait(t); norm=norm_of(t)
+        dg1[...]+=jnp.sum(da*norm,axis=1,keepdims=True)
+        ds1[...]+=jnp.sum(da,axis=1,keepdims=True)
+        e=da*g1[...]
+        eb[t]=e
+        stats.start(t,e,e*norm)
+    def last(t):
+        u,w=stats.wait(t)
+        in_ref[:,cols(t)]=dx1[:,cols(t)]+st[t,1:2]*(eb[t]-u-norm_of(t)*w)
+    for t in range(CH):
+        first(t)
+        if t: last(t-1)
+    last(CH-1)
+    out_copy.wait_recv()
+    o_out[...]=(dwo[:,lanes(c)].astype(f32)+yo[...].astype(f32)).astype(bf16)
+    q_copy.wait_recv()
+    for i in range(per):
+        q_out[i]=(tq[per*c+i].astype(f32)+yq[i].astype(f32)).astype(bf16)
+    out_copy.wait_send(); q_copy.wait_send()
+    for q in (total,stats): q.drain()
+
+def tail_block(dqkv,wq,a1,x,st,dx1,g1,dwo,ncol):
+    w,n=x.shape; T=n//CH; d=4*w; sd=jax.ShapeDtypeStruct; V=pltpu.VMEM
+    nq=wq.shape[1]; per=4//ncol; half=dwo.shape[1]//ncol
+    return pl.pallas_call(functools.partial(tail_kernel,ncol),name="tail_block",
+      out_shape=(sd((w,n),f32),sd((per,w,nq),bf16),sd((w,half),bf16),sd((w,1),f32),sd((w,1),f32)),
+      in_specs=[VM]*8,out_specs=(VM,)*5,
+      scratch_shapes=[V((CH,d,T),f32),V((1,CH,2,w,T),bf16),V((1,CH,2,w,T),bf16),V((1,CH,w,T),bf16),V((1,CH,w,T),bf16),
+        V((1,CH,8,T),f32),V((1,CH,3,8,T),f32),V((CH,w,T),f32),V((d,nq),bf16),V((4,w,nq),bf16),V((per,w,nq),bf16),V((w,half),bf16),
+        SEM((1,CH,4)),SEM((1,CH,6)),SEM((7,)),SEM((4,))],
+      cost_estimate=pl.CostEstimate(flops=2*10**9,bytes_accessed=10**8,transcendentals=0),
+      compiler_params=pltpu.CompilerParams(collective_id=3,has_side_effects=True,vmem_limit_bytes=56<<20),
+    )(dqkv,wq,a1,x,st,dx1,g1,dwo)
+
 def tiled(rows,step,body):
     def run(i,carry):
         body(pl.ds(pl.multiple_of(i*step,step),step))
@@ -345,8 +495,8 @@
         dst[:,i:i+step]=src[i:i+step,:].T
 
 def mlp_kernel(x_ref,cot_ref,o_ref,wo,wu,wd,bo,g2,s2,bu,bd,
-               y_ref,dx1_ref,do_ref,dwo_ref,dwd_ref,dwu_ref,dg2_ref,ds2_ref,dbo_ref,dbd_ref,dbu_ref,
-               wot,wut,wdt,part,part2,a2,dyb,dat,gb,dhb,x1b,st,da2b,s1b,r1b,s2b,r2b,tout,tgot,gsem,ssem,tsem):
+               y_ref,dx1_ref,do_ref,dwo_ref,dwd_ref,tup_ref,dg2_ref,ds2_ref,dbo_ref,dbd_ref,dbu_ref,
+               wot,wut,wdt,part,part2,a2,dyb,dat,gb,dhb,x1b,st,da2b,s1b,r1b,s2b,r2b,tout,tgot,dwu_ref,gsem,ssem,tsem,usem):
     p=Row(); T=x_ref.shape[1]//CH
     cols=lambda t:slice(T*t,T*(t+1))
     greet_row(p)
@@ -439,26 +589,28 @@
     for t in range(CH): dbd_ref[...]+=jnp.sum(cot_ref[:,cols(t)].astype(bf16).astype(f32),axis=1,keepdims=True)
     for t in range(CH): gd.forward(t)
     weight_grads()
+    turned=Turn(p,dwu_ref,tup_ref,usem)
     for t in range(CH): attended(t)
     acc=None
     for t in range(CH):
         v=nt(o_ref[T*t:T*(t+1),:].T,dat[t]); acc=v if acc is None else acc+v
     dwo_ref[...]=acc.astype(bf16)
     for t in range(CH): finish(t)
+    turned.wait()
     for c in (out_sum,y_sum,da_sum,ga,gy,gd,st2,stb): c.drain()
 
 def mlp_block(x,cot,o,wo,wu,wd,bo,g2,s2,bu,bd):
     w,n=x.shape; T=n//CH; hid=wu.shape[1]; d=wu.shape[0]
     sd=jax.ShapeDtypeStruct; V=pltpu.VMEM
     return pl.pallas_call(mlp_kernel,name="mlp_block",
-      out_shape=(sd((w,n),f32),sd((w,n),f32),sd((w,n),bf16),sd(wo.shape,bf16),sd((hid,d),bf16),sd((d,hid),bf16),
+      out_shape=(sd((w,n),f32),sd((w,n),f32),sd((w,n),bf16),sd(wo.shape,bf16),sd((hid,d),bf16),sd((4,w,hid),bf16),
                  sd((w,1),f32),sd((w,1),f32),sd((w,1),f32),sd((w,1),f32),sd((hid,1),f32)),
       in_specs=[VM]*11,out_specs=(VM,)*11,
       scratch_shapes=[V((d,w),bf16),V((hid,d),bf16),V((d,hid),bf16),V((CH,d,T),f32),V((CH,d,T),f32),
         V((CH,d,T),bf16),V((CH,d,T),bf16),V((CH,d,T),bf16),V((CH,hid,T),bf16),V((CH,hid,T),bf16),
         V((CH,w,T),f32),V((CH,8,T),f32),V((CH,w,T),f32),
         V((3,CH,2,w,T),bf16),V((3,CH,2,w,T),bf16),V((3,CH,w,T),bf16),V((3,CH,w,T),bf16),
-        V((2,CH,8,T),f32),V((2,CH,3,8,T),f32),SEM((3,CH,6)),SEM((3,CH,4)),SEM((2,CH,6))],
+        V((2,CH,8,T),f32),V((2,CH,3,8,T),f32),V((d,hid),bf16),SEM((3,CH,6)),SEM((3,CH,4)),SEM((2,CH,6)),SEM((7,))],
       cost_estimate=pl.CostEstimate(flops=8*10**9,bytes_accessed=3*10**7,transcendentals=10**6),
       compiler_params=pltpu.CompilerParams(collective_id=1,has_side_effects=True,vmem_limit_bytes=60<<20),
     )(x,cot,o,wo,wu,wd,bo,g2,s2,bu,bd)
@@ -474,10 +626,6 @@
         return [w[:,n*i:n*i+n].astype(bf16) for i in range(per)]
     qs=[head_order(a,b,c) for a,b,c in zip(quarters(q_weight),quarters(k_weight),quarters(v_weight))]
     us=quarters(up_weight)
-    own=jnp.stack([jnp.concatenate([a,b],1) for a,b in zip(qs,us)],1)
-    full=lax.all_gather(own,"col",axis=1,tiled=True)
-    turned=lax.all_to_all(full,"row",split_axis=1,concat_axis=0,tiled=True).reshape(D,-1)
-    w_qkv=turned[:,0:576]; w_up=turned[:,576:]
     w_out=gather_col(out_weight); w_down=gather_col(down_weight)
     col=lambda vec,n:own_rows(vec,n,r)[:,None]
     g1,s1,g2,s2=[col(v,width) for v in (ln1_gain,ln1_bias,ln2_gain,ln2_bias)]
@@ -486,33 +634,25 @@
     b_out,b_down=col(out_bias,width),col(down_bias,width); b_up=col(up_bias,hidden)
     rel=rel_operands(rel_pos_h,rel_pos_w)
     x=tokens
-    m,sq=row_stats(x,x*x)
-    inv1=lax.rsqrt(sq-m*m+EPS); norm1=(x-m)*inv1
-    a1=gather_rows((norm1*g1+s1).astype(bf16))
-    qkv=(tn(w_qkv,a1)+b_qkv).astype(bf16)
+    a1,qkv,w_qkv,w_up,st1=head_block(x,jnp.stack(qs),jnp.stack(us),g1,s1,b_qkv,cols)
+    w_qkv=w_qkv.reshape(D,-1); w_up=w_up.reshape(D,-1)
     o=attend(offsets,qkv,rel)
     output,dx1,do,d_out,d_down,d_up,d_g2,d_s2,d_out_bias,d_down_bias,d_up_bias=mlp_block(
         x,cotangent,o,w_out,w_up,w_down,b_out,g2,s2,b_up,b_down)
     d_g2,d_s2,d_out_bias,d_down_bias,d_up_bias=[v[:,0] for v in (d_g2,d_s2,d_out_bias,d_down_bias,d_up_bias)]
     dqkv,drel=attend_back(offsets,qkv,do,rel)
-    d_qkv=nn(a1,dqkv).astype(bf16)
     b_sums=head_unorder(jnp.sum(dqkv,axis=0,dtype=f32))
-    da1=sum_rows(nt(w_qkv,dqkv))
-    d_g1=jnp.sum(da1*norm1,axis=1); d_s1=jnp.sum(da1,axis=1)
-    e1=da1*g1
-    u,w=row_stats(e1,e1*norm1)
-    input_grad=dx1+inv1*(e1-u-norm1*w)
-    def turn_back(dw):
-        n=dw.shape[1]
-        t=lax.all_to_all(dw.reshape(rows,width,n),"row",split_axis=0,concat_axis=0,tiled=True)
-        return t
-    def reduce(t,axis):
-        return lax.psum(lax.psum_scatter(t,"col",scatter_dimension=axis,tiled=True),"dp").astype(f32)
-    t_up=reduce(turn_back(d_up),0); t_qkv=reduce(turn_back(d_qkv),0)
+    def reduce_col(t,axis): return lax.psum_scatter(t,"col",scatter_dimension=axis,tiled=True)
+    early=lax.psum((reduce_col(d_up,0),reduce_col(d_down,1)),"dp")
+    input_grad,t_qkv,t_out,d_g1,d_s1=tail_block(dqkv,w_qkv,a1,x,st1,dx1,g1,d_out,cols)
+    d_g1,d_s1=d_g1[:,0],d_s1[:,0]
+    early,(t_qkv,t_out)=lax.optimization_barrier((early,(t_qkv,t_out)))
+    t_qkv,t_out=lax.psum((t_qkv,t_out),"dp")
+    t_up,f_down=early[0].astype(f32),early[1].astype(f32)
+    f_out=t_out.astype(f32)
     f_up=jnp.concatenate([t_up[i] for i in range(per)],1)
-    parts=[head_unorder(t_qkv[i]) for i in range(per)]
-    f_q,f_k,f_v=[jnp.concatenate([p[i] for p in parts],1) for i in range(3)]
-    f_down=reduce(d_down,1); f_out=reduce(d_out,1)
+    parts=[head_unorder(t_qkv[i].astype(f32)) for i in range(per)]
+    f_q,f_k,f_v=[jnp.concatenate([q[i] for q in parts],1) for i in range(3)]
     dh_rel,dw_rel=rel_grads(drel)
     minor=lax.psum((spread(d_g1,D,r),spread(d_s1,D,r),spread(b_sums[0],D,r),spread(b_sums[2],D,r),dh_rel,dw_rel,
       spread(d_out_bias,D,r),spread(d_g2,D,r),spread(d_s2,D,r),spread(d_up_bias,up_bias.shape[0],r),spread(d_down_bias,D,r)),("dp","row","col"))

time: 429 us -> 397 us (0.925)
  Pallas kernels: 137 us -> 226 us
  waiting for transfers between devices: 108 us -> 45 us
  blocking collectives: 104 us -> 64.6 us
  matrix products: 9.63 us -> 0 us
    pallas_call x0 -> x2, Pallas kernels: none -> 77.6 us  [the longest x1 45.1 us: head_block(): pl.pallas_call(functools.partial(head_kernel, ncol), name='head_block', o...]
    all_to_all x2 -> x0, blocking collectives: 37.2 us -> none  [turn_back(): lax.all_to_all(dw.reshape(rows, width, n), 'row', split_axis=0, concat_ax...]
    psum x1 -> x2, waiting for transfers between devices: 26.1 us -> 0.02 us  [the longest x1 0.02 us: local(): early = lax.psum((reduce_col(d_up, 0), reduce_col(d_down, 1)), 'dp')]
    all_gather x2 -> x0, waiting for transfers between devices: 25.5 us -> none  [the longest x1 25.5 us: local(): full = lax.all_gather(own, 'col', axis=1, tiled=True)]
    unnamed x11 -> x6, waiting for transfers between devices: 0.17 us -> 22.9 us
    reduce_scatter x3 -> x1, waiting for transfers between devices: 43.4 us -> 22 us  [reduce_col(): return lax.psum_scatter(t, 'col', scatter_dimension=axis, tiled=True)]
    all_gather x1, blocking collectives: 6.91 us -> 22.5 us  [local(): lax.all_gather(w.astype(bf16), 'col', axis=1, tiled=True)]
    psum x2 -> x0, blocking collectives: 14.8 us -> none  [row_stats(): both = lax.psum(jnp.stack([jnp.sum(v, axis=0) for v in vals]), 'row')]
  transfers between devices with their start and end apart: 10 -> 5, of which waited for: 5 -> 2; matrix products, arithmetic and copies ran while one was open for 10% -> 7% of each run, Pallas kernels for 14% -> 34%
where the time goes in v3:
time: 397 us
  Pallas kernels  226 us (57%)
  blocking collectives  64.6 us (16%)
  waiting for transfers between devices  45 us (11%)
  local copies, waits for them, and re-layouts  30.5 us (8%)
  other arithmetic  15.4 us (4%)
  between operations  14.3 us (4%)
    pallas_call x1, Pallas kernels, mlp_block(): pl.pallas_call(mlp_kernel, name='mlp_block', out_shape=(sd((w, n), f32),...  90.3 us
    pallas_call x1, Pallas kernels, head_block(): pl.pallas_call(functools.partial(head_kernel, ncol), name='head_block', o...  45.1 us
    psum x1, blocking collectives, local(): lax.psum((spread(d_g1, D, r), spread(d_s1, D, r), spread(b_sums[0], D, r)...  42.1 us
    pallas_call x1, Pallas kernels, attend_back(): pl.pallas_call(bwd_kernel, out_shape=(jax.ShapeDtypeStruct((1024, 576), b...  41.1 us
    pallas_call x1, Pallas kernels, tail_block(): pl.pallas_call(functools.partial(tail_kernel, ncol), name='tail_block', o...  32.6 us
    unnamed x6, waiting for transfers between devices  22.9 us
    all_gather x1, blocking collectives, local(): lax.all_gather(w.astype(bf16), 'col', axis=1, tiled=True)  22.5 us
    reduce_scatter x1, waiting for transfers between devices, reduce_col(): return lax.psum_scatter(t, 'col', scatter_dimension=axis, tiled=True)  22 us
  transfers between devices with their start and end apart: 5, of which 2 were waited for; matrix products, arithmetic and copies ran while one was open for 7% of the time, Pallas kernels for 34%

profile of v3, /device:TPU:0, one launch (start us, length us, event | category | flops | bytes accessed | tf_op | source)
XLA Modules:
  0.0 396.5 jit_solution(7669148308445066653)
XLA Ops:
  7.3 2.2 convert_element_type.47
  9.6 0.8 copy-done.15
  10.7 0.8 dynamic_slice.29
  11.5 0.8 dynamic_slice.30
  12.5 0.8 dynamic_slice.27
  13.4 0.8 dynamic_slice.28
  14.8 0.8 dynamic_slice.31
  15.6 0.8 copy.61.bo
  16.4 0.8 dynamic_slice.32
  17.1 0.8 copy.62.g2
  17.9 0.8 dynamic_slice.33
  18.6 0.8 copy.63.s2
  19.4 0.8 dynamic_slice.35
  20.2 0.8 copy.65.bd
  21.0 0.8 dynamic_slice.34
  21.7 1.0 broadcast_in_dim.48.bu
  22.8 0.7 scatter.15
  24.0 0.7 scatter.19.rel
  25.5 1.0 copy-done.2
  26.5 45.1 %head_block.1 = (bf16[4,768,256]{2,1,0:T(8,128)(2,1)}, bf16[576,1024]{1,0:T(8,128)(2,1)S(1)}, bf16[4,192,576]{2,1,0:T(8,128)(2,1)S(1)}, bf16[4,192,768]{2,1,0:T(8,128)(2,1)S(1)}, f32[4,8,256]{2,1,0:T(8,128)S(1)}) custom-call(f32[192,1024]{1,0:T(8,128)S(1)} %copy-done.2, bf16[2,192,576]{2,1,0:T(8,128)(2,1)S(1)} %pad_maximum_fusion.2.oq_ref, ...), custom_call_target="tpu_custom_call" | custom-call | flops 1000000000 | bytes 100000000 | tf_op jit(solution)/shard_map/head_block/pallas_call | solution.py:411
  71.7 1.0 copy-done
  72.7 1.0 copy-done.3
  73.7 0.9 copy-done.4
  75.8 1.0 fusion.11.cells
  76.7 17.3 %attend.1.o_ref = bf16[1024,192]{1,0:T(8,128)(2,1)} custom-call(s32[1,2]{1,0:T(1,128)} %off.3, bf16[576,1024]{1,0:T(8,128)(2,1)} %copy-done, bf16[2,128,256]{2,1,0:T(8,128)(2,1)} %copy-done.7, s32[384,1]{1,0:T(8,128)} %fusion.11.cells, s32[1,256]{1,0:T(1,128)} %fusion.19.toks), custom_call_target="tpu_custom_call" | custom-call | tf_op jit(solution)/shard_map/attend/pallas_call | solution.py:128
  94.1 22.5 %all_gather.6.wo = bf16[192,768]{1,0:T(8,128)(2,1)} all-gather(bf16[192,384]{1,0:T(8,128)(2,1)S(1)} %convert_element_type.46), channel_id=1, replica_groups=mesh['dp'=4,'row'=4,'col'=2] {'col'}, dimensions={1}, use_global_device_ids=true | all-gather | bytes 442368 | tf_op jit(solution)/shard_map/all_gather | solution.py:622
  116.6 90.3 %mlp_block.1 = (f32[192,1024]{1,0:T(8,128)}, f32[192,1024]{1,0:T(8,128)}, bf16[192,1024]{1,0:T(8,128)(2,1)}, bf16[192,768]{1,0:T(8,128)(2,1)}, bf16[768,768]{1,0...) custom-call(f32[192,1024]{1,0:T(8,128)} %x_ref.5, ...), custom_call_target="tpu_custom_call" | custom-call | flops 8000000000 | bytes 30000000 | tf_op jit(solution)/shard_map/mlp_block/pallas_call | solution.py:605
  206.8 2.4 copy.69
  210.0 22.2 %reduce-scatter.7.cloned.1.call-done = bf16[384,768]{1,0:T(8,128)(2,1)} async-done(((bf16[768,768]{1,0:T(8,128)(2,1)}), bf16[384,768]{1,0:T(8,128)(2,1)}) %reduce-scatter.7.cloned.1.call-update) | async-done | bytes 589840
  232.2 2.1 copy.70
  234.3 22.0 %reduce-scatter.5.cloned.1.call-done = bf16[2,192,768]{2,1,0:T(8,128)(2,1)} async-done(((bf16[4,192,768]{2,1,0:T(8,128)(2,1)}), bf16[2,192,768]{2,1,0:T(8,128)(2,1)}) %reduce-scatter.5.cloned.1.call-update) | async-done | bytes 589840 | tf_op jit(solution)/shard_map/reduce_scatter | solution.py:645
  256.6 41.1 %attend_back.1 = (bf16[1024,576]{1,0:T(8,128)(2,1)}, f32[2,128,256]{2,1,0:T(8,128)}) custom-call(s32[1,2]{1,0:T(1,128)} %off.3, bf16[576,1024]{1,0:T(8,128)(2,1)} %copy-done, bf16[192,1024]{1,0:T(8,128)(2,1)} %get-tuple-element.97.do, bf16[2,128,256]{2,1,0:T(8,128)(2,1)} %copy-done.7, s32[384,1]{1,0:T(8,128)} %fusion.11.cells, s32[1,256]{1,0:T(1,128)} %fusion.19.toks), custom_call_target="tpu_custom_call" | custom-call | tf_op jit(solution)/shard_map/attend_back/pallas_call | solution.py:196
  297.8 1.6 convert_reduce_fusion
  299.5 32.6 %tail_block.1 = (f32[192,1024]{1,0:T(8,128)}, bf16[2,192,576]{2,1,0:T(8,128)(2,1)}, bf16[192,384]{1,0:T(8,128)(2,1)}, f32[192,1]{1,0:T(8,128)}, f32[192,1]{1,0:T(8,128)}) custom-call(bf16[1024,576]{1,0:T(8,128)(2,1)} %get-tuple-element.98.dqkv, bf16[768,576]{1,0:T(8,128)(2,1)} %bitcast.49, bf16[4,768,256]{2,1,0:T(8,128)(2,1)} %get-tuple-element.100.a1, ...), custom_call_target="tpu_custom_call" | custom-call | flops 2000000000 | bytes 100000000 | tf_op jit(solution)/shard_map/tail_block/pallas_call | solution.py:475
  332.4 1.1 reduce.8
  333.5 1.0 reduce.9
  337.0 42.1 %all-reduce.1 = (f32[768]{0:T(1024)}, f32[768]{0:T(1024)}, f32[768]{0:T(1024)}, f32[768]{0:T(1024)}, f32[27,64]{0,1:T(8,128)S(1)}, /*index=5*/f32[27,64]{0,1:T(8...) all-reduce(f32[768]{0:T(1024)S(1)} %dynamic_update_slice.27, ...), channel_id=1, replica_groups=mesh['dp'=4,'row'=4,'col'=2] {'dp','row','col'}, use_global_device_ids=true, to_apply=%region_0.0 | all-reduce | flops 12672 | bytes 101376 | tf_op jit(solution)/shard_map/psum | solution.py:657
  379.1 0.7 copy.67
  379.8 0.7 copy.68
  380.6 1.1 convert_element_type.55
  381.7 1.2 pad_maximum_fusion
  382.9 1.1 fusion.5
  384.9 0.7 convert_element_type.53
  385.7 0.9 pad_maximum_fusion.5
  386.5 0.9 pad_maximum_fusion.4
  387.4 0.9 pad_maximum_fusion.3
  388.2 0.9 copy.89
  389.1 0.9 copy.90
  (123 shorter events, 8.7 us)
Async XLA Ops:
  7.2 2.3 copy-start.13
  7.2 2.4 copy-start.14
  7.2 109.4 %all-gather.2.cloned.1.call-start = ((), (), s32[]{:S(2)}) async-start(), calls=%async_computation.2 | async-start | bytes 1769472 | tf_op jit(solution)/shard_map/all_gather | solution.py:622
  9.5 1.0 copy-start.15
  9.5 222.7 %reduce-scatter.7.cloned.1.call-start = ((), (), s32[]{:S(2)}) async-start(), calls=%async_computation.4 | async-start | bytes 1769472
  9.6 4.8 %copy-start.6 = (f32[192,1536]{1,0:T(8,128)S(1)}, f32[192,1536]{1,0:T(8,128)}, u32[]{:S(2)}) copy-start(f32[192,1536]{1,0:T(8,128)} %param.44) | copy-start | bytes 3538948
  10.7 3.7 copy-start.23
  12.3 2.4 copy-start.24
  13.4 12.1 %copy-start.1 = (f32[192,1]{1,0:T(8,128)}, f32[192,1]{1,0:T(8,128)S(1)}, u32[]{:S(2)}) copy-start(f32[192,1]{1,0:T(8,128)S(1)} %copy.56.g1) | copy-start | bytes 2308
  14.3 8.4 %copy-start.16 = (f32[192,384]{1,0:T(8,128)S(1)}, f32[192,384]{1,0:T(8,128)}, u32[]{:S(2)}) copy-start(f32[192,384]{1,0:T(8,128)} %param.40) | copy-start | bytes 884740
  24.8 0.7 copy-start.7
  25.4 1.1 copy-start.2
  71.6 1.0 copy-start
  72.7 1.0 copy-start.3
  73.7 0.9 copy-start.4
  74.6 0.6 copy-start.5
  209.2 47.1 %reduce-scatter.5.cloned.1.call-start = ((), (), s32[]{:S(2)}) async-start(), calls=%async_computation.3 | async-start | bytes 1769472 | tf_op jit(solution)/shard_map/reduce_scatter | solution.py:645
  210.0 122.3 %all-reduce.9.cloned.1.call-start = ((), (), s32[]{:S(2)}) async-start(), calls=%async_computation.6 | async-start | bytes 2359296 | tf_op jit(solution)/shard_map/psum | solution.py:646
  256.4 126.5 %all-reduce.7.cloned.1.call-start = ((), (), s32[]{:S(2)}) async-start(), calls=%async_computation.5 | async-start | bytes 1277952 | tf_op jit(solution)/shard_map/psum | solution.py:650
  299.5 32.6 %copy-start.22 = (f32[2,128,256]{2,1,0:T(8,128)S(1)}, f32[2,128,256]{2,1,0:T(8,128)}, u32[]{:S(2)}) copy-start(f32[2,128,256]{2,1,0:T(8,128)} %get-tuple-element.112) | copy-start | bytes 786436
  332.1 2.6 copy-start.12
  332.1 2.8 copy-start.21
  332.1 2.9 copy-start.20
  332.1 3.0 copy-start.19
  332.1 3.1 copy-start.18
  332.2 48.2 %copy-start.11 = (bf16[2,192,768]{2,1,0:T(8,128)(2,1)S(1)}, bf16[2,192,768]{2,1,0:T(8,128)(2,1)}, u32[]{:S(2)}) copy-start(bf16[2,192,768]{2,1,0:T(8,128)(2,1)} %get-tuple-element.117) | copy-start | bytes 1769476
  335.0 45.6 %copy-start.10 = (bf16[768,384]{1,0:T(8,128)(2,1)S(1)}, bf16[768,384]{1,0:T(8,128)(2,1)}, u32[]{:S(2)}) copy-start(bf16[768,384]{1,0:T(8,128)(2,1)} %get-tuple-element.119) | copy-start | bytes 1769476
  384.0 0.9 copy-start.17
  384.9 3.3 copy-start.8
  387.4 1.7 copy-start.9
Sparse Core Ops, SparseCore 0:
  10.1 25.4 all-gather.1
  209.4 22.8 reduce-scatter.6
  234.5 21.8 reduce-scatter.4
  259.2 56.0 all-reduce.8
  332.4 40.7 all-reduce.6
